TPU v7x, 32 devices: a whole 2x2x4 slice. The times are simulated.
32 devices in a mesh: replica: 2 (over x), yz: 4 (over z), x: 4 (over y, core).
Axes of the slice: x: 2, y: 2, z: 4, core: 2. Of those that a mesh axis runs over, the one named last changes fastest.
Arguments:
- hidden: bfloat16 [256, 4096], P('replica', ('x', 'yz')), parts along dimension 0
- seq_lens: int32 [256], P(('replica', 'yz', 'x')), parts along dimension 0
- attn_gain: bfloat16 [1, 4096], replicated
- mlp_gain: bfloat16 [1, 4096], replicated
- w_qkv: bfloat16 [1, 4096, 4352], P(None, None, 'yz')
- w_out: bfloat16 [1, 4096, 4096], P(None, 'yz')
- w_gate_up: bfloat16 [1, 4096, 2, 14336], P(None, None, None, 'yz')
- w_down: bfloat16 [1, 14336, 4096], P(None, 'yz')
- k_cache: bfloat16 [1, 256, 4096, 128], P(None, ('replica', 'yz', 'x')), parts along dimension 1
- v_cache: bfloat16 [1, 256, 4096, 128], P(None, ('replica', 'yz', 'x')), parts along dimension 1
Outputs:
- output 1: bfloat16 [256, 4096], P('replica', ('x', 'yz')), parts along dimension 0
- output 2: bfloat16 [1, 256, 4096, 128], P(None, ('replica', 'yz', 'x')), parts along dimension 1
- output 3: bfloat16 [1, 256, 4096, 128], P(None, ('replica', 'yz', 'x')), parts along dimension 1
There are 2 independent parts. A program takes and returns all parts, laid end to end along the dimension named above; an argument that names none is the same for every part.
All inputs are finite; a program needn't handle non-finite values.
Results may differ from a plain program's by a relative error of at most 0.0139522.
Values are sent between devices in bfloat16 or wider.
A program may use at most 1 GiB of HBM per device.

v0:
```python
import jax
import jax.numpy as jnp
from jax import lax
from jax.sharding import PartitionSpec as P

NORM_EPS = 1e-5


def attend(z_rows, k_layer, v_layer, seq_lens, head_dim):
    num_rows = z_rows.shape[0]
    attn_width = z_rows.shape[1] - 2 * head_dim
    num_heads = attn_width // head_dim
    queries = z_rows[:, :attn_width].reshape(num_rows, num_heads, head_dim)
    k_new = z_rows[:, attn_width:attn_width + head_dim]
    v_new = z_rows[:, attn_width + head_dim:]
    slot_ids = jnp.arange(k_layer.shape[1])
    at_slot = (slot_ids[None, :] == seq_lens[:, None])[:, :, None]
    k_upd = jnp.where(at_slot, k_new[:, None, :], k_layer)
    v_upd = jnp.where(at_slot, v_new[:, None, :], v_layer)
    scores = jnp.einsum('bhd,bsd->bhs', queries, k_upd, preferred_element_type=jnp.float32) * head_dim ** -0.5
    visible = (slot_ids[None, :] <= seq_lens[:, None])[:, None, :]
    scores = jnp.where(visible, scores, -1e30)
    probs_bf = jax.nn.softmax(scores, axis=-1).astype(jnp.bfloat16)
    outputs = jnp.einsum('bhs,bsd->bhd', probs_bf, v_upd, preferred_element_type=jnp.float32)
    return outputs.astype(jnp.bfloat16).reshape(num_rows, attn_width), k_upd, v_upd


def solution(mesh):
    group_axes = ('yz', 'x')
    batch_axes = ('replica', 'yz', 'x')
    hidden_spec = P('replica', ('x', 'yz'))
    cache_spec = P(None, batch_axes, None, None)
    x_size = mesh.shape['x']

    def norm_part(h_part, gain_part, model_dim):
        hid_f = h_part.astype(jnp.float32)
        sq_power = lax.psum(jnp.sum(hid_f * hid_f, axis=1, keepdims=True), 'x')
        inv_scale = lax.rsqrt(sq_power / model_dim + NORM_EPS)
        return (hid_f * inv_scale * gain_part.astype(jnp.float32)).astype(jnp.bfloat16)

    def residual(hidden, partial_sum):
        summed = lax.psum_scatter(partial_sum.astype(jnp.bfloat16), 'yz', scatter_dimension=1, tiled=True)
        return (hidden.astype(jnp.float32) + summed.astype(jnp.float32)).astype(jnp.bfloat16)

    def local_step(hidden, seq_lens, attn_gain, mlp_gain, w_qkv, w_out, w_gate_up, w_down, k_cache, v_cache):
        head_dim = k_cache.shape[-1]
        model_dim = attn_gain.shape[1] * x_size
        k_layers = []
        v_layers = []
        for layer_idx in range(w_qkv.shape[0]):
            gathered = lax.all_gather(hidden, 'yz', axis=1, tiled=True)
            normed = norm_part(gathered, attn_gain[layer_idx], model_dim)
            partial_z = jnp.dot(normed, w_qkv[layer_idx], preferred_element_type=jnp.float32).astype(jnp.bfloat16)
            z_cols = lax.psum_scatter(partial_z, 'x', scatter_dimension=1, tiled=True)
            z_rows = lax.all_to_all(z_cols, group_axes, 0, 1, tiled=True)
            attn_rows, k_upd, v_upd = attend(z_rows, k_cache[layer_idx], v_cache[layer_idx], seq_lens, head_dim)
            k_layers.append(k_upd)
            v_layers.append(v_upd)
            attn_cols = lax.all_to_all(attn_rows, group_axes, 1, 0, tiled=True)
            attn_slab = lax.all_gather(attn_cols, 'x', axis=1, tiled=True)
            hidden = residual(hidden, jnp.dot(attn_slab, w_out[layer_idx], preferred_element_type=jnp.float32))
            gathered = lax.all_gather(hidden, 'yz', axis=1, tiled=True)
            normed = norm_part(gathered, mlp_gain[layer_idx], model_dim)
            gu_part = jnp.einsum('be,etf->btf', normed, w_gate_up[layer_idx], preferred_element_type=jnp.float32).astype(jnp.bfloat16)
            gu_cols = lax.psum_scatter(gu_part, 'x', scatter_dimension=2, tiled=True)
            mlp_cols = (jax.nn.silu(gu_cols[:, 0].astype(jnp.float32)) * gu_cols[:, 1].astype(jnp.float32)).astype(jnp.bfloat16)
            mlp_slab = lax.all_gather(mlp_cols, 'x', axis=1, tiled=True)
            hidden = residual(hidden, jnp.dot(mlp_slab, w_down[layer_idx], preferred_element_type=jnp.float32))
        return hidden, jnp.stack(k_layers), jnp.stack(v_layers)

    return jax.shard_map(
        local_step,
        mesh=mesh,
        in_specs=(hidden_spec, P(batch_axes), P(None, 'x'), P(None, 'x'), P(None, 'x', 'yz'), P(None, 'yz', 'x'),
                  P(None, 'x', None, 'yz'), P(None, 'yz', 'x'), cache_spec, cache_spec),
        out_specs=(hidden_spec, cache_spec, cache_spec),
        check_vma=False)
```

profile of v0, /device:TPU:0, one launch (start us, length us, event | category | flops | bytes accessed | tf_op | source)
XLA Modules:
  0.0 239.3 jit_solution(18357255330545677989)
XLA Ops:
  7.2 1.2 dynamic-slice.7
  8.5 1.2 dynamic-slice
  10.3 15.5 %all_gather.12 = bf16[128,1024]{1,0:T(8,128)(2,1)S(1)} all-gather(bf16[128,256]{1,0:T(8,128)(2,1)} %param.10), channel_id=1, replica_groups=mesh['replica'=2,'yz'=4,'x'=4] {'yz'}, dimensions={1}, use_global_device_ids=true | all-gather | bytes 327680 | tf_op jit(solution)/shard_map/all_gather | solution.py:51
  26.0 5.7 %psum.14 = f32[128,1]{0,1:T(1,128)S(1)} all-reduce(f32[128,1]{0,1:T(1,128)S(1)} %bitcast.77), channel_id=1, replica_groups=mesh['replica'=2,'yz'=4,'x'=4] {'x'}, use_global_device_ids=true, to_apply=%region_1.0 | all-reduce | flops 128 | bytes 1024 | tf_op jit(solution)/shard_map/psum | solution.py:37
  32.4 3.8 %convolution_convert_fusion = bf16[128,1088]{0,1:T(8,128)(2,1)} fusion(bf16[1,4096,1088]{1,2,0:T(8,128)(2,1)} %param.14, s32[]{:T(128)} %bitcast.4, bf16[128,1024]{1,0:T(8,128)(2,1)S(1)} %all_gather.12, f32[1024]{0:T(1024)S(1)} %bitcast.75, f32[128]{0:T(128)S(1)} %rsqrt_bitcast_fusion.1), kind=kOutput, calls=%fused_computation.23 | convolution fusion | flops 285876224 | bytes 2774016 | tf_op jit(solution)/shard_map/dot_general | solution.py:53
  36.2 22.2 %reduce-scatter.7.cloned.1.call-done = bf16[128,272]{0,1:T(8,128)(2,1)} async-done(((bf16[128,1088]{0,1:T(8,128)(2,1)}), bf16[128,272]{0,1:T(8,128)(2,1)}) %reduce-scatter.7.cloned.1.call-update) | async-done | bytes 69648 | tf_op jit(solution)/shard_map/reduce_scatter | solution.py:54
  58.4 1.6 copy.18
  60.0 4.7 %all-to-all-start = ((bf16[16,8,272]{2,1,0:T(8,128)(2,1)}), bf16[16,8,272]{2,1,0:T(8,128)(2,1)S(1)}, u32[]{:S(2)}, u32[]{:S(2)}) async-start(bf16[16,8,272]{2,1,0:T(8,128)(2,1)} %bitcast.6), calls=%async_computation.1 | async-start | bytes 196608 | tf_op jit(solution)/shard_map/all_to_all | solution.py:55
  64.8 0.8 iota_compare_fusion.1
  65.6 6.4 %all-to-all-done = bf16[16,8,272]{2,1,0:T(8,128)(2,1)S(1)} async-done(((bf16[16,8,272]{2,1,0:T(8,128)(2,1)}), bf16[16,8,272]{2,1,0:T(8,128)(2,1)S(1)}, u32[]{:S(2)}, u32[]{:S(2)}) %all-to-all-start) | async-done | bytes 69664 | tf_op jit(solution)/shard_map/all_to_all | solution.py:55
  72.1 9.6 %fusion.17 = f32[8,32,4096]{2,1,0:T(8,128)S(1)} fusion(bf16[1,8,4096,128]{3,2,1,0:T(8,128)(2,1)} %param.18, pred[8,4096]{1,0:T(8,128)(4,1)S(1)} %get-tuple-element.10, bf16[8,128]{1,0:T(8,128)(2,1)S(1)} %get-tuple-element.5, pred[8,4096]{1,0:T(8,128)(4,1)S(1)} %get-tuple-element.9, bf16[1,8,32,128]{3,1,2,0:T(8,128)(2,1)S(1)} %slice_bitcast_fusion), kind=kOutput, calls=%fused_computation.19 | convolution fusion | flops 274726912 | bytes 12716032 | tf_op jit(solution)/shard_map/bhd,bsd->bhs/dot_general | solution.py:20
  81.7 2.0 copy-done
  83.7 0.8 fusion.59
  84.6 8.7 %fusion.32 = bf16[8,32,128]{2,1,0:T(8,128)(2,1)S(1)} fusion(bf16[1,8,4096,128]{3,2,1,0:T(8,128)(2,1)} %param.19, pred[8,4096]{1,0:T(8,128)(4,1)S(1)} %get-tuple-element.10, bf16[8,128]{1,0:T(8,128)(2,1)S(1)} %get-tuple-element.6, f32[8,32]{1,0:T(8,128)S(1)} %fusion.59, f32[8,32,4096]{2,1,0:T(8,128)} %copy-done), kind=kOutput, calls=%fused_computation.33 | convolution fusion | flops 275812608 | bytes 12684288 | tf_op jit(solution)/shard_map/bhs,bsd->bhd/dot_general | solution.py:24
  93.4 9.5 %all_to_all.38 = bf16[8,16,256]{2,0,1:T(8,128)(2,1)S(1)} all-to-all(bf16[8,16,256]{2,0,1:T(8,128)(2,1)S(1)} %copy.20), channel_id=1, replica_groups=mesh['replica'=2,'yz'=4,'x'=4] {'yz','x'}, dimensions={1} | all-to-all | bytes 131072 | tf_op jit(solution)/shard_map/all_to_all | solution.py:59
  102.8 5.8 %all_gather.13 = bf16[128,1024]{1,0:T(8,128)(2,1)S(1)} all-gather(bf16[128,256]{1,0:T(8,128)(2,1)S(1)} %bitcast.74), channel_id=1, replica_groups=mesh['replica'=2,'yz'=4,'x'=4] {'x'}, dimensions={1}, use_global_device_ids=true | all-gather | bytes 327680 | tf_op jit(solution)/shard_map/all_gather | solution.py:60
  108.6 3.4 %fusion.26 = bf16[128,1024]{1,0:T(8,128)(2,1)} fusion(bf16[128,1024]{1,0:T(8,128)(2,1)S(1)} %all_gather.13, bf16[1,1024,4096]{2,1,0:T(8,128)(2,1)} %param.15, s32[]{:T(128)} %bitcast.4), kind=kOutput, calls=%fused_computation.31 | convolution fusion | flops 268566528 | bytes 2621952 | tf_op jit(solution)/shard_map/dot_general | solution.py:61
  112.1 13.4 %constant_dynamic-slice_fusion = bf16[1,1024,2,3584]{3,2,1,0:T(2,128)(2,1)} fusion(bf16[1,4096,2,3584]{3,2,1,0:T(2,128)(2,1)} %param.16, s32[]{:T(128)} %bitcast.4), kind=kLoop, calls=%fused_computation.66 | loop fusion | bytes 29360132 | tf_op jit(solution)/call_exported
  126.2 3.2 %reduce-scatter.9.cloned.1.call-done = bf16[128,256]{1,0:T(8,128)(2,1)} async-done(((bf16[128,1024]{1,0:T(8,128)(2,1)}), bf16[128,256]{1,0:T(8,128)(2,1)}) %reduce-scatter.9.cloned.1.call-update) | async-done | bytes 65552 | tf_op jit(solution)/shard_map/reduce_scatter | solution.py:42
  129.4 0.9 add_convert_fusion.1
  130.2 13.8 %all_gather.14 = bf16[128,1024]{1,0:T(8,128)(2,1)S(1)} all-gather(bf16[128,256]{1,0:T(8,128)(2,1)S(1)} %add_convert_fusion.1), channel_id=1, replica_groups=mesh['replica'=2,'yz'=4,'x'=4] {'yz'}, dimensions={1}, use_global_device_ids=true | all-gather | bytes 327680 | tf_op jit(solution)/shard_map/all_gather | solution.py:62
  144.2 5.7 %psum.15 = f32[128,1]{0,1:T(1,128)S(1)} all-reduce(f32[128,1]{0,1:T(1,128)S(1)} %bitcast.78), channel_id=1, replica_groups=mesh['replica'=2,'yz'=4,'x'=4] {'x'}, use_global_device_ids=true, to_apply=%region_7.8 | all-reduce | flops 128 | bytes 1024 | tf_op jit(solution)/shard_map/psum | solution.py:37
  149.8 8.5 %fusion.14 = bf16[128,2,3584]{2,0,1:T(8,128)(2,1)} fusion(bf16[1,1024,2,3584]{3,2,1,0:T(2,128)(2,1)} %constant_dynamic-slice_fusion, bf16[128,1024]{1,0:T(8,128)(2,1)S(1)} %all_gather.14, f32[1024]{0:T(1024)S(1)} %bitcast.76, f32[128]{0:T(128)S(1)} %rsqrt_bitcast_fusion), kind=kOutput, calls=%fused_computation.18 | convolution fusion | flops 1880489984 | bytes 16781824 | tf_op jit(solution)/shard_map/be,etf->btf/dot_general | solution.py:64
  158.4 4.5 %copy.22 = bf16[128,2,3584]{0,1,2:T(2,128)(2,1)S(1)} copy(bf16[128,2,3584]{2,0,1:T(8,128)(2,1)} %fusion.14) | data formatting | bytes 3670016
  162.9 1.5 copy.39
  164.4 28.6 %reduce-scatter.13.cloned.1.call-done = bf16[896,256]{1,0:T(8,128)(2,1)} async-done(((bf16[3584,256]{1,0:T(8,128)(2,1)}), bf16[896,256]{1,0:T(8,128)(2,1)}) %reduce-scatter.13.cloned.1.call-update) | async-done | bytes 458768
  193.0 1.1 reshape.96
  196.3 8.7 %all_gather.15 = bf16[128,3584]{1,0:T(8,128)(2,1)S(1)} all-gather(bf16[128,896]{1,0:T(8,128)(2,1)S(1)} %fusion.43), channel_id=1, replica_groups=mesh['replica'=2,'yz'=4,'x'=4] {'x'}, dimensions={1}, use_global_device_ids=true | all-gather | bytes 1146880 | tf_op jit(solution)/shard_map/all_gather | solution.py:67
  205.0 5.5 %fusion.29 = bf16[128,1024]{1,0:T(8,128)(2,1)} fusion(bf16[128,3584]{1,0:T(8,128)(2,1)S(1)} %all_gather.15, bf16[1,3584,4096]{2,1,0:T(8,128)(2,1)} %param.17, s32[]{:T(128)} %bitcast.4), kind=kOutput, calls=%fused_computation.32 | convolution fusion | flops 939655168 | bytes 8520192 | tf_op jit(solution)/shard_map/dot_general | solution.py:68
  210.6 11.9 %broadcast_select_fusion = (bf16[1,8,4096,128]{3,2,1,0:T(8,128)(2,1)}, bf16[1,8,4096,128]{3,2,1,0:T(8,128)(2,1)}) fusion(bf16[1,8,4096,128]{3,2,1,0:T(8,128)(2,1)} %param.19, pred[8,4096]{1,0:T(8,128)(4,1)S(1)} %get-tuple-element.10, bf16[8,128]{1,0:T(8,128)(2,1)S(1)} %get-tuple-element.6, bf16[1,8,4096,128]{3,2,1,0:T(8,128)(2,1)} %param.18, ...), kind=kLoop, calls=%fused_computation.8 | loop fusion | flops 8388608 | bytes 33591296 | tf_op jit(solution)/shard_map/jit(_where)/select_n | solution.py:19
  222.4 8.8 %reduce-scatter.11.cloned.1.call-done = bf16[128,256]{1,0:T(8,128)(2,1)} async-done(((bf16[128,1024]{1,0:T(8,128)(2,1)}), bf16[128,256]{1,0:T(8,128)(2,1)}) %reduce-scatter.11.cloned.1.call-update) | async-done | bytes 65552 | tf_op jit(solution)/shard_map/reduce_scatter | solution.py:42
  231.3 1.5 add_convert_fusion
  (27 shorter events, 4.3 us)
Async XLA Ops:
  7.2 51.3 %reduce-scatter.7.cloned.1.call-start = ((), (), s32[]{:S(2)}) async-start(), calls=%async_computation.6 | async-start | bytes 348160 | tf_op jit(solution)/shard_map/reduce_scatter | solution.py:54
  60.0 11.9 %all-to-all-start = ((bf16[16,8,272]{2,1,0:T(8,128)(2,1)}), bf16[16,8,272]{2,1,0:T(8,128)(2,1)S(1)}, u32[]{:S(2)}, u32[]{:S(2)}) async-start(bf16[16,8,272]{2,1,0:T(8,128)(2,1)} %bitcast.6), calls=%async_computation.1 | async-start | bytes 196608 | tf_op jit(solution)/shard_map/all_to_all | solution.py:55
  64.8 64.6 %reduce-scatter.9.cloned.1.call-start = ((), (), s32[]{:S(2)}) async-start(), calls=%async_computation.7 | async-start | bytes 327680 | tf_op jit(solution)/shard_map/reduce_scatter | solution.py:42
  81.7 2.0 copy-start
  112.0 17.4 %copy-start.1 = (bf16[128,256]{1,0:T(8,128)(2,1)S(1)}, bf16[128,256]{1,0:T(8,128)(2,1)}, u32[]{:S(2)}) copy-start(bf16[128,256]{1,0:T(8,128)(2,1)} %param.10) | copy-start | bytes 196612
  112.0 80.9 %reduce-scatter.13.cloned.1.call-start = ((), (), s32[]{:S(2)}) async-start(), calls=%async_computation.9 | async-start | bytes 2293760
  164.4 66.9 %reduce-scatter.11.cloned.1.call-start = ((), (), s32[]{:S(2)}) async-start(), calls=%async_computation.8 | async-start | bytes 327680 | tf_op jit(solution)/shard_map/reduce_scatter | solution.py:42
Sparse Core Ops, SparseCore 0:
  36.3 22.0 reduce-scatter.6
  112.1 17.1 reduce-scatter.8
  164.5 28.4 reduce-scatter.12
  210.7 20.5 reduce-scatter.10
where the time goes:
time: 240 us; the launch traced here: 239 us
  waiting for transfers between devices  69.2 us (29%)
  blocking collectives  64.5 us (27%)
  matrix products  39.6 us (16%)
  local copies, waits for them, and re-layouts  28.9 us (12%)
  other arithmetic  17.6 us (7%)
  between operations  14.6 us (6%)
  starting transfers between devices  4.88 us (2%)
    all_gather x2, blocking collectives, local_step(): gathered = lax.all_gather(hidden, 'yz', axis=1, tiled=True)  29.3 us
    unnamed x5, waiting for transfers between devices  28.6 us
    reduce_scatter x1, waiting for transfers between devices, local_step(): z_cols = lax.psum_scatter(partial_z, 'x', scatter_dimension=1, tiled=True)  22.2 us
    another operation x3, local copies, waits for them, and re-layouts  15.9 us
    reduce_scatter x2, waiting for transfers between devices, residual(): lax.psum_scatter(partial_sum.astype(jnp.bfloat16), 'yz', scatter_dimensio...  12 us
    select_n x1, other arithmetic, attend(): v_upd = jnp.where(at_slot, v_new[:, None, :], v_layer)  11.9 us
    psum x2, blocking collectives, norm_part(): sq_power = lax.psum(jnp.sum(hid_f * hid_f, axis=1, keepdims=True), 'x')  11.3 us
    unnamed x10, local copies, waits for them, and re-layouts  10.5 us
  transfers between devices with their start and end apart: 5, of which 5 were waited for; matrix products, arithmetic and copies ran while one was open for 11% of the time, Pallas kernels for 0%

commit v1 on v0

v1 whole, which is shorter than its diff:
```python
import functools

import jax
import jax.numpy as jnp
from jax import lax
from jax.experimental import pallas as pl
from jax.experimental.pallas import tpu as pltpu
from jax.sharding import PartitionSpec as P

NORM_EPS = 1e-5
MESH = pl.DeviceIdType.MESH
BF = jnp.bfloat16
F32 = jnp.float32
MIB = 1024 * 1024


def at(z, x):
    return {"yz": z, "x": x}


def remote(src, dst, ssem, rsem, z, x):
    return pltpu.make_async_remote_copy(src_ref=src, dst_ref=dst, send_sem=ssem, recv_sem=rsem,
                                        device_id=at(z, x), device_id_type=MESH)


def group_barrier(z, x):
    sem = pltpu.get_barrier_semaphore()
    me = z * 4 + x

    def body(p, c):
        d = lax.rem(me + p, 16)
        pl.semaphore_signal(sem, inc=1, device_id=at(lax.div(d, 4), lax.rem(d, 4)), device_id_type=MESH)
        return c

    lax.fori_loop(1, 16, body, 0)
    pl.semaphore_wait(sem, 15)


def by_distance(z):
    a, b = lax.div(z, 2), lax.rem(z, 2)
    first = lax.div(z + 3, 4)
    n1 = first * (z - 1) + (1 - first)
    n2 = 2 + a * (1 - 2 * b)
    return n1, n2, 6 - z - n1 - n2


def gather(buf, slot, src_for, ssem, rsem, z, x):
    yx = lax.rem(x + 2, 4)
    cx = x + 1 - 2 * lax.rem(x, 2)
    cyx = lax.rem(cx + 2, 4)
    near = by_distance(z)
    me = slot(z, x)
    started = []

    def send(src, s, zt, xt):
        cp = remote(src, buf.at[s], ssem.at[len(started)], rsem.at[s], zt, xt)
        cp.start()
        started.append(cp)

    def arrived(s):
        remote(buf.at[s], buf.at[s], ssem.at[0], rsem.at[s], z, x).wait_recv()

    send(src_for(z), me, z, yx)
    for zt in near:
        send(src_for(zt), me, zt, x)
    send(src_for(z), me, z, cx)
    s = slot(z, yx)
    arrived(s)
    send(buf.at[s], s, z, cx)
    for zt in near:
        s = slot(zt, x)
        arrived(s)
        send(buf.at[s], s, z, yx)
        send(buf.at[s], s, z, cx)
    for zt in near:
        s = slot(zt, yx)
        arrived(s)
        send(buf.at[s], s, z, cx)
    for zt in (z, *near):
        arrived(slot(zt, cx))
        arrived(slot(zt, cyx))
    return started


def norm_scale(hb, count):
    def body(g, tot):
        h = hb[g].astype(F32)
        return tot + jnp.sum(h * h, axis=1, keepdims=True)

    tot = lax.fori_loop(0, count, body, jnp.zeros((hb.shape[1], 1), F32))
    return lax.rsqrt(tot / (count * hb.shape[2]) + NORM_EPS)


def normed(hb, gain_ref, g, r):
    w = hb.shape[2]
    gain = gain_ref[:, pl.ds(pl.multiple_of(g * w, w), w)].astype(F32)
    return (hb[g].astype(F32) * r * gain).astype(BF)


def qkv_kernel(h_ref, gain_ref, w_hbm, out_ref, hb, wbuf, acc, zloc, zbuf, wsem, ssem, rsem, ssem2, rsem2):
    z, x = lax.axis_index("yz"), lax.axis_index("x")
    me = z * 4 + x
    parts = [
        pltpu.make_async_copy(w_hbm.at[0, pl.ds(pl.multiple_of(x * 256, 256), 256), :], wbuf.at[pl.ds(0, 256), :], wsem.at[0]),
        pltpu.make_async_copy(w_hbm.at[0, pl.ds(1024, 64), :], wbuf.at[pl.ds(256, 64), :], wsem.at[1]),
        pltpu.make_async_copy(w_hbm.at[0, pl.ds(1024, 64), :], wbuf.at[pl.ds(320, 64), :], wsem.at[2]),
    ]
    for cp in parts:
        cp.start()
    group_barrier(z, x)
    hb[x * 4 + z] = h_ref[...]
    sent = gather(hb, lambda zt, xt: xt * 4 + zt, lambda zt: h_ref, ssem, rsem, z, x)
    r = norm_scale(hb, 16)
    acc[...] = jnp.zeros_like(acc)
    for cp in parts:
        cp.wait()

    def body(g, c):
        u = normed(hb, gain_ref, g, r)
        w = wbuf[:, pl.ds(pl.multiple_of(g * 256, 256), 256)]
        acc[...] += lax.dot_general(u, w, (((1,), (1,)), ((), ())), preferred_element_type=F32)
        return c

    lax.fori_loop(0, 16, body, 0)
    for d in range(16):
        zloc[d] = acc[d * 8:(d + 1) * 8, :].astype(BF)

    def peer(p):
        d = lax.rem(me + p, 16)
        return remote(zloc.at[d], zbuf.at[me], ssem2.at[p], rsem2.at[me], lax.div(d, 4), lax.rem(d, 4))

    def start(p, c):
        peer(p).start()
        return c

    def finish(p, c):
        peer(p).wait_send()
        d = lax.rem(me + p, 16)
        remote(zbuf.at[d], zbuf.at[d], ssem2.at[0], rsem2.at[d], z, x).wait_recv()
        return c

    lax.fori_loop(1, 16, start, 0)
    zbuf[me] = zloc[me]
    for cp in sent:
        cp.wait_send()
    lax.fori_loop(1, 16, finish, 0)
    out_ref[...] = zbuf[...]


def attn_kernel(len_ref, z_ref, k_hbm, v_hbm, o_ref, ko_hbm, vo_hbm, kbuf, vbuf, zrow, orow, isem, osem):
    rows, positions, hd = kbuf.shape

    def load(b, which):
        if which == 0:
            return pltpu.make_async_copy(k_hbm.at[0, b], kbuf.at[b], isem.at[0, b])
        return pltpu.make_async_copy(v_hbm.at[0, b], vbuf.at[b], isem.at[1, b])

    def store(b, which):
        if which == 0:
            return pltpu.make_async_copy(kbuf.at[b], ko_hbm.at[0, b], osem.at[0, b])
        return pltpu.make_async_copy(vbuf.at[b], vo_hbm.at[0, b], osem.at[1, b])

    def start(b, c):
        load(b, 0).start()
        load(b, 1).start()
        return c

    lax.fori_loop(0, rows, start, 0)
    lane = lax.broadcasted_iota(jnp.int32, (rows, hd), 1)
    for pair in range(2):
        base = 17 * pair
        even, odd = 8 * pair, 8 * pair + 4
        mains_e = [z_ref[even + i // 2, :, (i % 2) * hd:(i % 2 + 1) * hd].astype(F32) for i in range(8)]
        mains_o = [pltpu.roll(z_ref[odd + i // 2, :, (i % 2) * hd:(i % 2 + 1) * hd].astype(F32), hd // 2, 1) for i in range(8)]
        tail_e = z_ref[even, :, 2 * hd:3 * hd].astype(F32)
        tail_o = z_ref[odd, :, 2 * hd:3 * hd].astype(F32)
        heads = mains_e + [jnp.where(lane < hd // 2, tail_e, mains_o[0])]
        for i in range(8):
            heads.append(jnp.where(lane < hd // 2, mains_o[i], mains_o[i + 1] if i < 7 else tail_o))
        for i, v in enumerate(heads):
            zrow[:, base + i, :] = v
    heads = zrow.shape[1] - 2
    scale = hd ** -0.5

    def put(buf, b, row, pos):
        lo = pl.multiple_of(lax.div(pos, 16) * 16, 16)
        tile = buf[b, pl.ds(lo, 16), :].astype(F32)
        hit = lax.broadcasted_iota(jnp.int32, (16, hd), 0) == pos - lo
        buf[b, pl.ds(lo, 16), :] = jnp.where(hit, row, tile).astype(BF)

    def body(b, c):
        pos = len_ref[b]
        load(b, 0).wait()
        put(kbuf, b, zrow[b, heads:heads + 1, :], pos)
        q = zrow[b, 0:heads, :].astype(BF)
        s = lax.dot_general(q, kbuf[b], (((1,), (1,)), ((), ())), preferred_element_type=F32) * scale
        ids = lax.broadcasted_iota(jnp.int32, s.shape, 1)
        s = jnp.where(ids <= pos, s, -1e30)
        e = jnp.exp(s - jnp.max(s, axis=1, keepdims=True))
        p = (e / jnp.sum(e, axis=1, keepdims=True)).astype(BF)
        load(b, 1).wait()
        put(vbuf, b, zrow[b, heads + 1:heads + 2, :], pos)
        orow[b] = jnp.dot(p, vbuf[b], preferred_element_type=F32)
        store(b, 0).start()
        store(b, 1).start()
        return c

    lax.fori_loop(0, rows, body, 0)
    for h in range(heads):
        o_ref[h // 8, h % 8] = orow[:, h, :].astype(BF)

    def finish(b, c):
        store(b, 0).wait()
        store(b, 1).wait()
        return c

    lax.fori_loop(0, rows, finish, 0)


def mlp_kernel(o_ref, h_ref, gain_ref, wo_hbm, wg_hbm, wd_hbm, out_ref,
               wo, wg, wd, spread, obuf, olhs, part, recv, hb, acc, mbuf, part2, recv2,
               wsem, ssem_o, rsem_o, ssem_p, rsem_p, ssem_h, rsem_h, ssem_m, rsem_m, ssem_q, rsem_q):
    z, x = lax.axis_index("yz"), lax.axis_index("x")
    cols = pl.ds(pl.multiple_of(x * 1024, 1024), 1024)
    tiles = wg.shape[0]
    depth = wg.shape[1]
    flat = wg_hbm.at[0].reshape(depth, wg_hbm.shape[3])
    loads = [pltpu.make_async_copy(wo_hbm.at[0, :, cols], wo, wsem.at[0])]
    for j in range(tiles):
        lanes = pl.ds(pl.multiple_of((x * tiles + j) * 128, 128), 128)
        loads.append(pltpu.make_async_copy(flat.at[:, lanes], wg.at[j], wsem.at[1 + j]))
    loads.append(pltpu.make_async_copy(wd_hbm.at[0, :, cols], wd, wsem.at[1 + tiles]))
    for cp in loads:
        cp.start()
    group_barrier(z, x)

    k_id = lax.broadcasted_iota(jnp.int32, (256, 512), 0)
    c_id = lax.broadcasted_iota(jnp.int32, (256, 512), 1)
    spread[0] = jnp.where(c_id == 2 * k_id, 1.0, 0.0).astype(BF)
    spread[1] = jnp.where(c_id == 2 * k_id + 1, 1.0, 0.0).astype(BF)

    obuf[z * 4 + x] = o_ref[z]
    sent = gather(obuf, lambda zt, xt: zt * 4 + xt, lambda zt: o_ref.at[zt], ssem_o, rsem_o, z, x)
    for h in range(8):
        olhs[:, h * 128:(h + 1) * 128] = obuf[:, h].reshape(128, 128)

    def reduce_scatter(product, part, recv, ssem, rsem):
        copies = []
        for i, zt in enumerate(by_distance(z)):
            part[zt] = product(zt).astype(BF)
            cp = remote(part.at[zt], recv.at[z], ssem.at[i], rsem.at[z], zt, x)
            cp.start()
            copies.append(cp)
        total = product(z)
        for zt in by_distance(z):
            remote(recv.at[zt], recv.at[zt], ssem.at[0], rsem.at[zt], z, x).wait_recv()
            total += recv[zt].astype(F32)
        return total, copies

    loads[0].wait()

    def out_block(zt):
        return jnp.dot(olhs[...], wo[:, pl.ds(pl.multiple_of(zt * 256, 256), 256)], preferred_element_type=F32)

    total, more = reduce_scatter(out_block, part, recv, ssem_p, rsem_p)
    sent += more
    own = x * 4 + z
    hb[own] = (h_ref[...].astype(F32) + total).astype(BF)
    sent += gather(hb, lambda zt, xt: xt * 4 + zt, lambda zt: hb.at[own], ssem_h, rsem_h, z, x)
    r = norm_scale(hb, 16)
    acc[...] = jnp.zeros_like(acc)
    for j in range(tiles):
        loads[1 + j].wait()

    def body(g, c):
        u = normed(hb, gain_ref, g, r)
        even = jnp.dot(u, spread[0], preferred_element_type=F32).astype(BF)
        odd = jnp.dot(u, spread[1], preferred_element_type=F32).astype(BF)
        lhs = jnp.concatenate([even, odd], axis=0)
        rows = pl.ds(pl.multiple_of(g * 512, 512), 512)
        for j in range(0, tiles, 2):
            width = min(2, tiles - j)
            w = jnp.concatenate([wg[j + i, rows, :] for i in range(width)], axis=1)
            acc[:, j * 128:(j + width) * 128] += jnp.dot(lhs, w, preferred_element_type=F32)
        return c

    lax.fori_loop(0, 16, body, 0)
    gate = acc[0:128, :].astype(BF).astype(F32)
    up = acc[128:256, :].astype(BF).astype(F32)
    mbuf[x] = (jax.nn.silu(gate) * up).astype(BF)

    yx = lax.rem(x + 2, 4)
    cx = x + 1 - 2 * lax.rem(x, 2)
    cyx = lax.rem(cx + 2, 4)
    mcopies = [remote(mbuf.at[x], mbuf.at[x], ssem_m.at[0], rsem_m.at[x], z, yx),
               remote(mbuf.at[x], mbuf.at[x], ssem_m.at[1], rsem_m.at[x], z, cx)]
    for cp in mcopies:
        cp.start()
    remote(mbuf.at[yx], mbuf.at[yx], ssem_m.at[0], rsem_m.at[yx], z, x).wait_recv()
    cp = remote(mbuf.at[yx], mbuf.at[yx], ssem_m.at[2], rsem_m.at[yx], z, cx)
    cp.start()
    sent += mcopies + [cp]
    for xt in (cx, cyx):
        remote(mbuf.at[xt], mbuf.at[xt], ssem_m.at[0], rsem_m.at[xt], z, x).wait_recv()
    loads[1 + tiles].wait()

    def down_block(zt):
        lanes = pl.ds(pl.multiple_of(zt * 256, 256), 256)
        width = mbuf.shape[2]
        return functools.reduce(lambda a, b: a + b, [
            jnp.dot(mbuf[i], wd[i * width:(i + 1) * width, lanes], preferred_element_type=F32) for i in range(4)])

    total, more = reduce_scatter(down_block, part2, recv2, ssem_q, rsem_q)
    sent += more
    out_ref[...] = (hb[own].astype(F32) + total).astype(BF)
    for cp in sent:
        cp.wait_send()


def solution(mesh):
    hidden_spec = P('replica', ('x', 'yz'))
    batch_axes = ('replica', 'yz', 'x')
    cache_spec = P(None, batch_axes, None, None)
    vmem = pl.BlockSpec(memory_space=pltpu.VMEM)
    smem = pl.BlockSpec(memory_space=pltpu.SMEM)
    anywhere = pl.BlockSpec(memory_space=pl.ANY)
    dma, sd = pltpu.SemaphoreType.DMA, jax.ShapeDtypeStruct

    def layer(hidden, seq_lens, attn_gain, mlp_gain, w_qkv, w_out, w_gate_up, w_down, k_cache, v_cache):
        w_qkv_t = jnp.swapaxes(w_qkv, 1, 2)
        z_rows = pl.pallas_call(
            qkv_kernel,
            out_shape=sd((16, 8, 384), BF),
            in_specs=[vmem, vmem, anywhere],
            out_specs=vmem,
            scratch_shapes=[pltpu.VMEM((16, 128, 256), BF), pltpu.VMEM((384, 4096), BF), pltpu.VMEM((128, 384), F32),
                            pltpu.VMEM((16, 8, 384), BF), pltpu.VMEM((16, 8, 384), BF),
                            dma((3,)), dma((15,)), dma((16,)), dma((16,)), dma((16,))],
            compiler_params=pltpu.CompilerParams(collective_id=0, has_side_effects=True, vmem_limit_bytes=16 * MIB),
            name="qkv",
        )(hidden, attn_gain, w_qkv_t)
        rows, positions, hd = k_cache.shape[1:]
        o, k_out, v_out = pl.pallas_call(
            attn_kernel,
            out_shape=(sd((4, 8, rows, hd), BF), sd(k_cache.shape, BF), sd(v_cache.shape, BF)),
            in_specs=[smem, vmem, anywhere, anywhere],
            out_specs=(vmem, anywhere, anywhere),
            scratch_shapes=[pltpu.VMEM((rows, positions, hd), BF), pltpu.VMEM((rows, positions, hd), BF),
                            pltpu.VMEM((rows, 34, hd), F32), pltpu.VMEM((rows, 32, hd), F32),
                            dma((2, rows)), dma((2, rows))],
            compiler_params=pltpu.CompilerParams(vmem_limit_bytes=32 * MIB),
            name="attend",
        )(seq_lens, z_rows, k_cache, v_cache)
        hidden = pl.pallas_call(
            mlp_kernel,
            out_shape=sd(hidden.shape, BF),
            in_specs=[vmem, vmem, vmem, anywhere, anywhere, anywhere],
            out_specs=vmem,
            scratch_shapes=[pltpu.VMEM((1024, 1024), BF), pltpu.VMEM((7, 8192, 128), BF), pltpu.VMEM((3584, 1024), BF),
                            pltpu.VMEM((2, 256, 512), BF), pltpu.VMEM((16, 8, 8, 128), BF), pltpu.VMEM((128, 1024), BF),
                            pltpu.VMEM((4, 128, 256), BF), pltpu.VMEM((4, 128, 256), BF), pltpu.VMEM((16, 128, 256), BF),
                            pltpu.VMEM((256, 896), F32), pltpu.VMEM((4, 128, 896), BF),
                            pltpu.VMEM((4, 128, 256), BF), pltpu.VMEM((4, 128, 256), BF),
                            dma((9,)), dma((15,)), dma((16,)), dma((3,)), dma((4,)), dma((15,)), dma((16,)),
                            dma((3,)), dma((4,)), dma((3,)), dma((4,))],
            compiler_params=pltpu.CompilerParams(collective_id=1, has_side_effects=True, vmem_limit_bytes=56 * MIB),
            name="mlp",
        )(o, hidden, mlp_gain, w_out, w_gate_up, w_down)
        return hidden, k_out, v_out

    return jax.shard_map(
        layer,
        mesh=mesh,
        in_specs=(hidden_spec, P(batch_axes), P(), P(), P(None, None, 'yz'), P(None, 'yz', None),
                  P(None, None, None, 'yz'), P(None, 'yz', None), cache_spec, cache_spec),
        out_specs=(hidden_spec, cache_spec, cache_spec),
        check_vma=False)
```

time: 240 us -> 110 us (0.46)
  Pallas kernels: 0 us -> 98.2 us
  waiting for transfers between devices: 69.2 us -> 0 us
  blocking collectives: 64.5 us -> 0 us
  matrix products: 39.6 us -> 0 us
  local copies, waits for them, and re-layouts: 28.9 us -> 10.6 us
  other arithmetic: 17.6 us -> 0 us
  between operations: 14.6 us -> 0.71 us
  starting transfers between devices: 4.88 us -> 0 us
    pallas_call x0 -> x3, Pallas kernels: none -> 98.2 us  [the longest x1 58.4 us: layer(): pl.pallas_call(mlp_kernel, out_shape=sd(hidden.shape, BF), in_specs=[vmem...]
    all_gather x4 -> x0, blocking collectives: 43.7 us -> none  [the longest x2 29.3 us: local_step(): gathered = lax.all_gather(hidden, 'yz', axis=1, tiled=True)]
    dot_general x6 -> x0, matrix products: 39.6 us -> none  [the longest x1 9.58 us: attend(): jnp.einsum('bhd,bsd->bhs', queries, k_upd, preferred_element_type=jnp.flo...]
    reduce_scatter x3 -> x0, waiting for transfers between devices: 34.2 us -> none  [the longest x1 22.2 us: local_step(): z_cols = lax.psum_scatter(partial_z, 'x', scatter_dimension=1, tiled=True)]
    unnamed x5 -> x0, waiting for transfers between devices: 28.6 us -> none
    another operation x3 -> x0, local copies, waits for them, and re-layouts: 15.9 us -> none
    select_n x1 -> x0, other arithmetic: 11.9 us -> none  [attend(): v_upd = jnp.where(at_slot, v_new[:, None, :], v_layer)]
    psum x2 -> x0, blocking collectives: 11.3 us -> none  [norm_part(): sq_power = lax.psum(jnp.sum(hid_f * hid_f, axis=1, keepdims=True), 'x')]
  transfers between devices with their start and end apart: 5 -> 0, of which waited for: 5 -> 0; matrix products, arithmetic and copies ran while one was open for 11% -> 0% of each run, Pallas kernels for 0% -> 0%
where the time goes in v1:
time: 110 us
  Pallas kernels  98.2 us (89%)
  local copies, waits for them, and re-layouts  10.6 us (10%)
    pallas_call x1, Pallas kernels, layer(): pl.pallas_call(mlp_kernel, out_shape=sd(hidden.shape, BF), in_specs=[vmem...  58.4 us
    pallas_call x1, Pallas kernels, layer(): pl.pallas_call(qkv_kernel, out_shape=sd((16, 8, 384), BF), in_specs=[vmem...  28.6 us
    pallas_call x1, Pallas kernels, layer(): pl.pallas_call(attn_kernel, out_shape=(sd((4, 8, rows, hd), BF), sd(k_cac...  11.2 us
    unnamed x15, local copies, waits for them, and re-layouts  10.6 us

profile of v1, /device:TPU:0, one launch (start us, length us, event | category | flops | bytes accessed | tf_op | source)
XLA Modules:
  0.0 109.5 jit_solution(14715487212034564456)
XLA Ops:
  0.6 0.0 copy-start.6
  0.6 0.0 copy-start
  0.7 3.5 %copy-done = bf16[1,4096,1088]{1,2,0:T(8,128)(2,1)S(1)} copy-done((bf16[1,4096,1088]{1,2,0:T(8,128)(2,1)S(1)}, bf16[1,4096,1088]{1,2,0:T(8,128)(2,1)}, u32[]{:S(2)}) %copy-start) | copy-done | bytes 8912920
  4.2 0.0 copy-start.3
  4.2 0.8 copy-done.3
  5.0 0.0 copy-start.5
  5.0 0.7 copy-done.5
  5.7 0.0 copy-start.1
  5.7 28.6 %qkv.1.z_ref = bf16[16,8,384]{2,1,0:T(8,128)(2,1)S(1)} custom-call(bf16[128,256]{1,0:T(8,128)(2,1)S(1)} %copy-done.3, bf16[1,4096]{1,0:T(2,128)(2,1)S(1)} %copy-done.5, bf16[1,1088,4096]{2,1,0:T(8,128)(2,1)S(1)} %bitcast.1), custom_call_target="tpu_custom_call" | custom-call | tf_op jit(solution)/shard_map/qkv/pallas_call | solution.py:331
  34.4 0.0 copy-done.6
  34.4 0.0 copy-done.1
  34.4 0.0 copy-start.2
  34.4 3.4 %copy-done.2 = bf16[1,8,4096,128]{3,2,1,0:T(8,128)(2,1)S(1)} copy-done((bf16[1,8,4096,128]{3,2,1,0:T(8,128)(2,1)S(1)}, bf16[1,8,4096,128]{3,2,1,0:T(8,128)(2,1)}, u32[]{:S(2)}) %copy-start.2) | copy-done | bytes 8388632
  37.8 11.2 %attend.1 = (bf16[4,8,8,128]{3,2,1,0:T(8,128)(2,1)S(1)}, bf16[1,8,4096,128]{3,2,1,0:T(8,128)(2,1)}, bf16[1,8,4096,128]{3,2,1,0:T(8,128)(2,1)}) custom-call(s32[8]{0:T(128)S(1)} %copy-done.6, bf16[16,8,384]{2,1,0:T(8,128)(2,1)S(1)} %qkv.1.z_ref, bf16[1,8,4096,128]{3,2,1,0:T(8,128)(2,1)S(1)} %copy-done.1, bf16[1,8,4096,128]{3,2,1,0:T(8,128)(2,1)S(1)} %copy-done.2), custom_call_target="tpu_custom_call" | custom-call | tf_op jit(solution)/shard_map/attend/pallas_call | solution.py:343
  49.0 0.0 copy-start.4
  49.0 0.6 copy-done.4
  49.6 58.4 %mlp.1 = bf16[128,256]{1,0:T(8,128)(2,1)} custom-call(bf16[4,8,8,128]{3,2,1,0:T(8,128)(2,1)} %copy-done.4, bf16[128,256]{1,0:T(8,128)(2,1)} %h_ref.3, bf16[1,4096]{1,0:T(2,128)(2,1)} %gain_ref.3, bf16[1,1024,4096]{2,1,0:T(8,128)(2,1)} %wo_hbm.1, bf16[1,4096,2,3584]{3,2,1,0:T(2,128)(2,1)} %wg_hbm.1, bf16[1,3584,4096]{2,1,0:T(8,128)(2,1)} %wd_hbm.1), custom_call_target="tpu_custom_call" | custom-call | tf_op jit(solution)/shard_map/mlp/pallas_call | solution.py:354
  108.0 1.5 %copy.14 = bf16[128,256]{1,0:T(8,128)(2,1)} copy(bf16[128,256]{1,0:T(8,128)(2,1)} %mlp.1) | data formatting | bytes 131072
Async XLA Ops:
  0.6 33.7 %copy-start.6 = (s32[8]{0:T(128)S(1)}, s32[8]{0:T(128)}, u32[]{:S(2)}) copy-start(s32[8]{0:T(128)} %len_ref.1) | copy-start | bytes 100
  0.6 3.5 %copy-start = (bf16[1,4096,1088]{1,2,0:T(8,128)(2,1)S(1)}, bf16[1,4096,1088]{1,2,0:T(8,128)(2,1)}, u32[]{:S(2)}) copy-start(bf16[1,4096,1088]{1,2,0:T(8,128)(2,1)} %param.14) | copy-start | bytes 26738692
  4.2 0.8 copy-start.3
  5.0 0.7 copy-start.5
  5.7 28.7 %copy-start.1 = (bf16[1,8,4096,128]{3,2,1,0:T(8,128)(2,1)S(1)}, bf16[1,8,4096,128]{3,2,1,0:T(8,128)(2,1)}, u32[]{:S(2)}) copy-start(bf16[1,8,4096,128]{3,2,1,0:T(8,128)(2,1)} %k_hbm.1) | copy-start | bytes 25165828
  34.4 3.4 %copy-start.2 = (bf16[1,8,4096,128]{3,2,1,0:T(8,128)(2,1)S(1)}, bf16[1,8,4096,128]{3,2,1,0:T(8,128)(2,1)}, u32[]{:S(2)}) copy-start(bf16[1,8,4096,128]{3,2,1,0:T(8,128)(2,1)} %v_hbm.1) | copy-start | bytes 25165828
  49.0 0.6 copy-start.4

commit v2 on v1

--- a/solution.py
+++ b/solution.py
@@ -12,6 +12,7 @@
 BF = jnp.bfloat16
 F32 = jnp.float32
 MIB = 1024 * 1024
+UNROLL = 2
 
 
 def at(z, x):
@@ -44,11 +45,11 @@
     return n1, n2, 6 - z - n1 - n2
 
 
-def gather(buf, slot, src_for, ssem, rsem, z, x):
+def gather(buf, slot, src_for, ssem, rsem, z, x, ready=None, consume=None):
     yx = lax.rem(x + 2, 4)
     cx = x + 1 - 2 * lax.rem(x, 2)
     cyx = lax.rem(cx + 2, 4)
-    near = by_distance(z)
+    n1, n2, n3 = near = by_distance(z)
     me = slot(z, x)
     started = []
 
@@ -60,35 +61,75 @@
     def arrived(s):
         remote(buf.at[s], buf.at[s], ssem.at[0], rsem.at[s], z, x).wait_recv()
 
+    def pass_on(zt, xt, *targets):
+        s = slot(zt, xt)
+        arrived(s)
+        for t in targets:
+            send(buf.at[s], s, z, t)
+
+    def work(first, second, *late):
+        for zt, xt in late:
+            arrived(slot(zt, xt))
+        if consume is not None:
+            s0, s1 = slot(*first), slot(*second)
+            lax.fori_loop(0, 2, lambda i, c: (consume(s0 + i * (s1 - s0)), c)[1], 0)
+
     send(src_for(z), me, z, yx)
     for zt in near:
         send(src_for(zt), me, zt, x)
     send(src_for(z), me, z, cx)
-    s = slot(z, yx)
-    arrived(s)
-    send(buf.at[s], s, z, cx)
-    for zt in near:
-        s = slot(zt, x)
-        arrived(s)
-        send(buf.at[s], s, z, yx)
-        send(buf.at[s], s, z, cx)
-    for zt in near:
-        s = slot(zt, yx)
-        arrived(s)
-        send(buf.at[s], s, z, cx)
-    for zt in (z, *near):
-        arrived(slot(zt, cx))
-        arrived(slot(zt, cyx))
+    pass_on(z, yx, cx)
+    pass_on(n1, x, yx, cx)
+    if ready is not None:
+        ready()
+    work((z, x), (z, yx))
+    pass_on(n2, x, yx, cx)
+    work((n1, x), (z, cx), (z, cx))
+    pass_on(n3, x, yx, cx)
+    work((n2, x), (z, cyx), (z, cyx))
+    pass_on(n1, yx, cx)
+    work((n3, x), (n1, cx), (n1, cx))
+    pass_on(n2, yx, cx)
+    work((n1, yx), (n2, cx), (n2, cx))
+    work((n2, yx), (n3, cx), (n3, cx))
+    pass_on(n3, yx, cx)
+    work((n3, yx), (n1, cyx), (n1, cyx))
+    work((n2, cyx), (n3, cyx), (n2, cyx), (n3, cyx))
     return started
 
 
-def norm_scale(hb, count):
-    def body(g, tot):
-        h = hb[g].astype(F32)
-        return tot + jnp.sum(h * h, axis=1, keepdims=True)
-
-    tot = lax.fori_loop(0, count, body, jnp.zeros((hb.shape[1], 1), F32))
-    return lax.rsqrt(tot / (count * hb.shape[2]) + NORM_EPS)
+def share_sums(h, stat, ssem, rsem, z, x):
+    me = z * 4 + x
+    rows = h.shape[0]
+    hf = h.astype(F32)
+    sums = jnp.broadcast_to(jnp.sum(hf * hf, axis=1, keepdims=True), (rows, 128))
+    stat[me] = jnp.transpose(sums)[0:1, :]
+
+    def peer(p):
+        d = lax.rem(me + p, 16)
+        return remote(stat.at[me], stat.at[me], ssem.at[p], rsem.at[me], lax.div(d, 4), lax.rem(d, 4))
+
+    def start(p, c):
+        peer(p).start()
+        return c
+
+    lax.fori_loop(1, 16, start, 0)
+    return peer
+
+
+def scale_of(stat, peer, ssem, rsem, z, x, width):
+    me = z * 4 + x
+
+    def finish(p, c):
+        peer(p).wait_send()
+        d = lax.rem(me + p, 16)
+        remote(stat.at[d], stat.at[d], ssem.at[0], rsem.at[d], z, x).wait_recv()
+        return c
+
+    lax.fori_loop(1, 16, finish, 0)
+    tot = functools.reduce(lambda u, v: u + v, [stat[i] for i in range(16)])
+    r = lax.rsqrt(tot / width + NORM_EPS)
+    return jnp.transpose(jnp.broadcast_to(r, (128, 128)))[:, 0:1]
 
 
 def normed(hb, gain_ref, g, r):
@@ -97,7 +138,8 @@
     return (hb[g].astype(F32) * r * gain).astype(BF)
 
 
-def qkv_kernel(h_ref, gain_ref, w_hbm, out_ref, hb, wbuf, acc, zloc, zbuf, wsem, ssem, rsem, ssem2, rsem2):
+def qkv_kernel(h_ref, gain_ref, w_hbm, out_ref, hb, wbuf, acc, scale, stat, zloc, zbuf,
+               wsem, ssem, rsem, ssem_s, rsem_s, ssem2, rsem2):
     z, x = lax.axis_index("yz"), lax.axis_index("x")
     me = z * 4 + x
     parts = [
@@ -107,21 +149,22 @@
     ]
     for cp in parts:
         cp.start()
+    hb[x * 4 + z] = h_ref[...]
+    acc[...] = jnp.zeros_like(acc)
     group_barrier(z, x)
-    hb[x * 4 + z] = h_ref[...]
-    sent = gather(hb, lambda zt, xt: xt * 4 + zt, lambda zt: h_ref, ssem, rsem, z, x)
-    r = norm_scale(hb, 16)
-    acc[...] = jnp.zeros_like(acc)
-    for cp in parts:
-        cp.wait()
-
-    def body(g, c):
-        u = normed(hb, gain_ref, g, r)
+    peer_s = share_sums(h_ref[...], stat, ssem_s, rsem_s, z, x)
+
+    def ready():
+        scale[...] = scale_of(stat, peer_s, ssem_s, rsem_s, z, x, 4096)
+        for cp in parts:
+            cp.wait()
+
+    def consume(g):
+        u = normed(hb, gain_ref, g, scale[...])
         w = wbuf[:, pl.ds(pl.multiple_of(g * 256, 256), 256)]
         acc[...] += lax.dot_general(u, w, (((1,), (1,)), ((), ())), preferred_element_type=F32)
-        return c
-
-    lax.fori_loop(0, 16, body, 0)
+
+    sent = gather(hb, lambda zt, xt: xt * 4 + zt, lambda zt: h_ref, ssem, rsem, z, x, ready, consume)
     for d in range(16):
         zloc[d] = acc[d * 8:(d + 1) * 8, :].astype(BF)
 
@@ -147,22 +190,23 @@
     out_ref[...] = zbuf[...]
 
 
-def attn_kernel(len_ref, z_ref, k_hbm, v_hbm, o_ref, ko_hbm, vo_hbm, kbuf, vbuf, zrow, orow, isem, osem):
-    rows, positions, hd = kbuf.shape
-
-    def load(b, which):
-        if which == 0:
-            return pltpu.make_async_copy(k_hbm.at[0, b], kbuf.at[b], isem.at[0, b])
-        return pltpu.make_async_copy(v_hbm.at[0, b], vbuf.at[b], isem.at[1, b])
+def attn_kernel(len_ref, z_ref, k_ref, v_ref, o_ref, ko_hbm, vo_hbm, zrow, orow, tiles, osem, tsem):
+    rows, positions, hd = k_ref.shape[1:]
 
     def store(b, which):
-        if which == 0:
-            return pltpu.make_async_copy(kbuf.at[b], ko_hbm.at[0, b], osem.at[0, b])
-        return pltpu.make_async_copy(vbuf.at[b], vo_hbm.at[0, b], osem.at[1, b])
+        src, dst = ((k_ref, ko_hbm), (v_ref, vo_hbm))[which]
+        return pltpu.make_async_copy(src.at[0, b], dst.at[0, b], osem.at[which, b])
+
+    def first(b):
+        return pl.multiple_of(lax.div(len_ref[b], 16) * 16, 16)
+
+    def patch(b, which):
+        dst = (ko_hbm, vo_hbm)[which]
+        return pltpu.make_async_copy(tiles.at[which, b], dst.at[0, b, pl.ds(first(b), 16), :], tsem.at[which, b])
 
     def start(b, c):
-        load(b, 0).start()
-        load(b, 1).start()
+        store(b, 0).start()
+        store(b, 1).start()
         return c
 
     lax.fori_loop(0, rows, start, 0)
@@ -180,46 +224,59 @@
         for i, v in enumerate(heads):
             zrow[:, base + i, :] = v
     heads = zrow.shape[1] - 2
-    scale = hd ** -0.5
-
-    def put(buf, b, row, pos):
-        lo = pl.multiple_of(lax.div(pos, 16) * 16, 16)
-        tile = buf[b, pl.ds(lo, 16), :].astype(F32)
+    factor = hd ** -0.5 * 1.4426950408889634
+
+    def updated(ref, b, row, pos):
+        lo = first(b)
+        tile = ref[0, b, pl.ds(lo, 16), :].astype(F32)
         hit = lax.broadcasted_iota(jnp.int32, (16, hd), 0) == pos - lo
-        buf[b, pl.ds(lo, 16), :] = jnp.where(hit, row, tile).astype(BF)
-
-    def body(b, c):
+        return jnp.where(hit, row, tile).astype(BF)
+
+    def one(b):
         pos = len_ref[b]
-        load(b, 0).wait()
-        put(kbuf, b, zrow[b, heads:heads + 1, :], pos)
-        q = zrow[b, 0:heads, :].astype(BF)
-        s = lax.dot_general(q, kbuf[b], (((1,), (1,)), ((), ())), preferred_element_type=F32) * scale
+        k_new, v_new = zrow[b, heads:heads + 1, :], zrow[b, heads + 1:heads + 2, :]
+        tiles[0, b] = updated(k_ref, b, k_new, pos)
+        tiles[1, b] = updated(v_ref, b, v_new, pos)
+        q = zrow[b, 0:heads, :]
+        s = lax.dot_general(q.astype(BF), k_ref[0, b], (((1,), (1,)), ((), ())), preferred_element_type=F32)
+        s_new = jnp.sum(q * k_new, axis=1, keepdims=True)
         ids = lax.broadcasted_iota(jnp.int32, s.shape, 1)
-        s = jnp.where(ids <= pos, s, -1e30)
-        e = jnp.exp(s - jnp.max(s, axis=1, keepdims=True))
-        p = (e / jnp.sum(e, axis=1, keepdims=True)).astype(BF)
-        load(b, 1).wait()
-        put(vbuf, b, zrow[b, heads + 1:heads + 2, :], pos)
-        orow[b] = jnp.dot(p, vbuf[b], preferred_element_type=F32)
-        store(b, 0).start()
-        store(b, 1).start()
-        return c
-
-    lax.fori_loop(0, rows, body, 0)
+        s = jnp.where(ids < pos, s, -1e30)
+        top = jnp.maximum(jnp.max(s, axis=1, keepdims=True), s_new)
+        e = jnp.exp2((s - top) * factor)
+        e_new = jnp.exp2((s_new - top) * factor)
+        inv = 1.0 / (jnp.sum(e, axis=1, keepdims=True) + e_new)
+        p = (e * inv).astype(BF)
+        p_new = (e_new * inv).astype(BF).astype(F32)
+        orow[b] = jnp.dot(p, v_ref[0, b], preferred_element_type=F32) + p_new * v_new
+
+    def body(i, c):
+        for k in range(UNROLL):
+            one(i * UNROLL + k)
+        return c
+
+    lax.fori_loop(0, rows // UNROLL, body, 0)
     for h in range(heads):
         o_ref[h // 8, h % 8] = orow[:, h, :].astype(BF)
 
+    def fix(b, c):
+        for which in range(2):
+            store(b, which).wait()
+            patch(b, which).start()
+        return c
+
     def finish(b, c):
-        store(b, 0).wait()
-        store(b, 1).wait()
-        return c
-
+        for which in range(2):
+            patch(b, which).wait()
+        return c
+
+    lax.fori_loop(0, rows, fix, 0)
     lax.fori_loop(0, rows, finish, 0)
 
 
 def mlp_kernel(o_ref, h_ref, gain_ref, wo_hbm, wg_hbm, wd_hbm, out_ref,
-               wo, wg, wd, spread, obuf, olhs, part, recv, hb, acc, mbuf, part2, recv2,
-               wsem, ssem_o, rsem_o, ssem_p, rsem_p, ssem_h, rsem_h, ssem_m, rsem_m, ssem_q, rsem_q):
+               wo, wg, wd, spread, obuf, olhs, part, recv, hb, acc, scale, stat, mbuf, part2, recv2,
+               wsem, ssem_s, rsem_s, ssem_o, rsem_o, ssem_p, rsem_p, ssem_h, rsem_h, ssem_m, rsem_m, ssem_q, rsem_q):
     z, x = lax.axis_index("yz"), lax.axis_index("x")
     cols = pl.ds(pl.multiple_of(x * 1024, 1024), 1024)
     tiles = wg.shape[0]
@@ -266,14 +323,16 @@
     sent += more
     own = x * 4 + z
     hb[own] = (h_ref[...].astype(F32) + total).astype(BF)
-    sent += gather(hb, lambda zt, xt: xt * 4 + zt, lambda zt: hb.at[own], ssem_h, rsem_h, z, x)
-    r = norm_scale(hb, 16)
+    peer_s = share_sums(hb[own], stat, ssem_s, rsem_s, z, x)
     acc[...] = jnp.zeros_like(acc)
-    for j in range(tiles):
-        loads[1 + j].wait()
-
-    def body(g, c):
-        u = normed(hb, gain_ref, g, r)
+
+    def ready():
+        scale[...] = scale_of(stat, peer_s, ssem_s, rsem_s, z, x, 4096)
+        for j in range(tiles):
+            loads[1 + j].wait()
+
+    def consume(g):
+        u = normed(hb, gain_ref, g, scale[...])
         even = jnp.dot(u, spread[0], preferred_element_type=F32).astype(BF)
         odd = jnp.dot(u, spread[1], preferred_element_type=F32).astype(BF)
         lhs = jnp.concatenate([even, odd], axis=0)
@@ -282,9 +341,8 @@
             width = min(2, tiles - j)
             w = jnp.concatenate([wg[j + i, rows, :] for i in range(width)], axis=1)
             acc[:, j * 128:(j + width) * 128] += jnp.dot(lhs, w, preferred_element_type=F32)
-        return c
-
-    lax.fori_loop(0, 16, body, 0)
+
+    sent += gather(hb, lambda zt, xt: xt * 4 + zt, lambda zt: hb.at[own], ssem_h, rsem_h, z, x, ready, consume)
     gate = acc[0:128, :].astype(BF).astype(F32)
     up = acc[128:256, :].astype(BF).astype(F32)
     mbuf[x] = (jax.nn.silu(gate) * up).astype(BF)
@@ -323,7 +381,7 @@
     cache_spec = P(None, batch_axes, None, None)
     vmem = pl.BlockSpec(memory_space=pltpu.VMEM)
     smem = pl.BlockSpec(memory_space=pltpu.SMEM)
-    anywhere = pl.BlockSpec(memory_space=pl.ANY)
+    hbm = pl.BlockSpec(memory_space=pltpu.HBM)
     dma, sd = pltpu.SemaphoreType.DMA, jax.ShapeDtypeStruct
 
     def layer(hidden, seq_lens, attn_gain, mlp_gain, w_qkv, w_out, w_gate_up, w_down, k_cache, v_cache):
@@ -331,37 +389,39 @@
         z_rows = pl.pallas_call(
             qkv_kernel,
             out_shape=sd((16, 8, 384), BF),
-            in_specs=[vmem, vmem, anywhere],
+            in_specs=[vmem, vmem, hbm],
             out_specs=vmem,
             scratch_shapes=[pltpu.VMEM((16, 128, 256), BF), pltpu.VMEM((384, 4096), BF), pltpu.VMEM((128, 384), F32),
+                            pltpu.VMEM((128, 1), F32), pltpu.VMEM((16, 1, 128), F32),
                             pltpu.VMEM((16, 8, 384), BF), pltpu.VMEM((16, 8, 384), BF),
-                            dma((3,)), dma((15,)), dma((16,)), dma((16,)), dma((16,))],
-            compiler_params=pltpu.CompilerParams(collective_id=0, has_side_effects=True, vmem_limit_bytes=16 * MIB),
+                            dma((3,)), dma((15,)), dma((16,)), dma((16,)), dma((16,)), dma((16,)), dma((16,))],
+            compiler_params=pltpu.CompilerParams(collective_id=0, has_side_effects=True, vmem_limit_bytes=46 * MIB),
+            cost_estimate=pl.CostEstimate(flops=30_000_000_000, bytes_accessed=20_000_000, transcendentals=0),
             name="qkv",
         )(hidden, attn_gain, w_qkv_t)
         rows, positions, hd = k_cache.shape[1:]
         o, k_out, v_out = pl.pallas_call(
             attn_kernel,
             out_shape=(sd((4, 8, rows, hd), BF), sd(k_cache.shape, BF), sd(v_cache.shape, BF)),
-            in_specs=[smem, vmem, anywhere, anywhere],
-            out_specs=(vmem, anywhere, anywhere),
-            scratch_shapes=[pltpu.VMEM((rows, positions, hd), BF), pltpu.VMEM((rows, positions, hd), BF),
-                            pltpu.VMEM((rows, 34, hd), F32), pltpu.VMEM((rows, 32, hd), F32),
-                            dma((2, rows)), dma((2, rows))],
-            compiler_params=pltpu.CompilerParams(vmem_limit_bytes=32 * MIB),
+            in_specs=[smem, vmem, vmem, vmem],
+            out_specs=(vmem, hbm, hbm),
+            scratch_shapes=[pltpu.VMEM((rows, 34, hd), F32), pltpu.VMEM((rows, 32, hd), F32),
+                            pltpu.VMEM((2, rows, 16, hd), BF), dma((2, rows)), dma((2, rows))],
+            compiler_params=pltpu.CompilerParams(vmem_limit_bytes=28 * MIB),
             name="attend",
         )(seq_lens, z_rows, k_cache, v_cache)
         hidden = pl.pallas_call(
             mlp_kernel,
             out_shape=sd(hidden.shape, BF),
-            in_specs=[vmem, vmem, vmem, anywhere, anywhere, anywhere],
+            in_specs=[vmem, vmem, vmem, hbm, hbm, hbm],
             out_specs=vmem,
             scratch_shapes=[pltpu.VMEM((1024, 1024), BF), pltpu.VMEM((7, 8192, 128), BF), pltpu.VMEM((3584, 1024), BF),
                             pltpu.VMEM((2, 256, 512), BF), pltpu.VMEM((16, 8, 8, 128), BF), pltpu.VMEM((128, 1024), BF),
                             pltpu.VMEM((4, 128, 256), BF), pltpu.VMEM((4, 128, 256), BF), pltpu.VMEM((16, 128, 256), BF),
-                            pltpu.VMEM((256, 896), F32), pltpu.VMEM((4, 128, 896), BF),
+                            pltpu.VMEM((256, 896), F32), pltpu.VMEM((128, 1), F32), pltpu.VMEM((16, 1, 128), F32),
+                            pltpu.VMEM((4, 128, 896), BF),
                             pltpu.VMEM((4, 128, 256), BF), pltpu.VMEM((4, 128, 256), BF),
-                            dma((9,)), dma((15,)), dma((16,)), dma((3,)), dma((4,)), dma((15,)), dma((16,)),
+                            dma((9,)), dma((16,)), dma((16,)), dma((15,)), dma((16,)), dma((3,)), dma((4,)), dma((15,)), dma((16,)),
                             dma((3,)), dma((4,)), dma((3,)), dma((4,))],
             compiler_params=pltpu.CompilerParams(collective_id=1, has_side_effects=True, vmem_limit_bytes=56 * MIB),
             name="mlp",

time: 110 us -> 91 us (0.83)
  Pallas kernels: 98.2 us -> 86.4 us
  local copies, waits for them, and re-layouts: 10.6 us -> 3.66 us
    unnamed x15 -> x13, local copies, waits for them, and re-layouts: 10.6 us -> 3.66 us
    pallas_call x1, Pallas kernels: 58.4 us -> 52.2 us  [layer(): pl.pallas_call(mlp_kernel, out_shape=sd(hidden.shape, BF), in_specs=[vmem...]
    pallas_call x1, Pallas kernels: 28.6 us -> 25.2 us  [layer(): pl.pallas_call(qkv_kernel, out_shape=sd((16, 8, 384), BF), in_specs=[vmem...]
    pallas_call x1, Pallas kernels: 11.2 us -> 9.01 us  [layer(): pl.pallas_call(attn_kernel, out_shape=(sd((4, 8, rows, hd), BF), sd(k_cac...]
where the time goes in v2:
time: 91 us; the launch traced here: 90.7 us
  Pallas kernels  86.4 us (95%)
  local copies, waits for them, and re-layouts  3.66 us (4%)
    pallas_call x1, Pallas kernels, layer(): pl.pallas_call(mlp_kernel, out_shape=sd(hidden.shape, BF), in_specs=[vmem...  52.2 us
    pallas_call x1, Pallas kernels, layer(): pl.pallas_call(qkv_kernel, out_shape=sd((16, 8, 384), BF), in_specs=[vmem...  25.2 us
    pallas_call x1, Pallas kernels, layer(): pl.pallas_call(attn_kernel, out_shape=(sd((4, 8, rows, hd), BF), sd(k_cac...  9.01 us
    unnamed x13, local copies, waits for them, and re-layouts  3.66 us

profile of v2, /device:TPU:0, one launch (start us, length us, event | category | flops | bytes accessed | tf_op | source)
XLA Modules:
  0.0 90.7 jit_solution(15628089578702682181)
XLA Ops:
  0.6 0.0 copy-start.2
  0.6 0.8 copy-done.2
  1.5 0.0 copy-start.5
  1.5 0.7 copy-done.5
  2.2 0.0 copy-start
  2.2 0.0 copy-start.1
  2.2 0.0 copy-start.4
  2.2 25.2 %qkv.1.z_ref = bf16[16,8,384]{2,1,0:T(8,128)(2,1)S(1)} custom-call(bf16[128,256]{1,0:T(8,128)(2,1)S(1)} %copy-done.2, bf16[1,4096]{1,0:T(2,128)(2,1)S(1)} %copy-done.5, bf16[1,1088,4096]{2,1,0:T(8,128)(2,1)} %bitcast.1), custom_call_target="tpu_custom_call" | custom-call | flops 30000001024 | bytes 20000000 | tf_op jit(solution)/shard_map/qkv/pallas_call | solution.py:389
  27.4 0.0 copy-done
  27.4 0.0 copy-done.1
  27.4 0.0 copy-done.4
  27.4 9.0 %attend.1 = (bf16[4,8,8,128]{3,2,1,0:T(8,128)(2,1)S(1)}, bf16[1,8,4096,128]{3,2,1,0:T(8,128)(2,1)}, bf16[1,8,4096,128]{3,2,1,0:T(8,128)(2,1)}) custom-call(s32[8]{0:T(128)S(1)} %copy-done.4, bf16[16,8,384]{2,1,0:T(8,128)(2,1)S(1)} %qkv.1.z_ref, bf16[1,8,4096,128]{3,2,1,0:T(8,128)(2,1)S(1)} %copy-done, bf16[1,8,4096,128]{3,2,1,0:T(8,128)(2,1)S(1)} %copy-done.1), custom_call_target="tpu_custom_call" | custom-call | tf_op jit(solution)/shard_map/attend/pallas_call | solution.py:403
  36.4 0.0 copy-start.3
  36.5 0.6 copy-done.3
  37.1 52.2 %mlp.1 = bf16[128,256]{1,0:T(8,128)(2,1)} custom-call(bf16[4,8,8,128]{3,2,1,0:T(8,128)(2,1)} %copy-done.3, bf16[128,256]{1,0:T(8,128)(2,1)} %h_ref.3, bf16[1,4096]{1,0:T(2,128)(2,1)} %gain_ref.3, bf16[1,1024,4096]{2,1,0:T(8,128)(2,1)} %wo_hbm.1, bf16[1,4096,2,3584]{3,2,1,0:T(2,128)(2,1)} %wg_hbm.1, bf16[1,3584,4096]{2,1,0:T(8,128)(2,1)} %wd_hbm.1), custom_call_target="tpu_custom_call" | custom-call | tf_op jit(solution)/shard_map/mlp/pallas_call | solution.py:413
  89.3 1.5 %copy.14 = bf16[128,256]{1,0:T(8,128)(2,1)} copy(bf16[128,256]{1,0:T(8,128)(2,1)} %mlp.1) | data formatting | bytes 131072
Async XLA Ops:
  0.6 0.8 copy-start.2
  1.5 0.7 copy-start.5
  2.2 25.2 %copy-start = (bf16[1,8,4096,128]{3,2,1,0:T(8,128)(2,1)S(1)}, bf16[1,8,4096,128]{3,2,1,0:T(8,128)(2,1)}, u32[]{:S(2)}) copy-start(bf16[1,8,4096,128]{3,2,1,0:T(8,128)(2,1)} %k_ref.1) | copy-start | bytes 25165828
  2.2 25.2 %copy-start.1 = (bf16[1,8,4096,128]{3,2,1,0:T(8,128)(2,1)S(1)}, bf16[1,8,4096,128]{3,2,1,0:T(8,128)(2,1)}, u32[]{:S(2)}) copy-start(bf16[1,8,4096,128]{3,2,1,0:T(8,128)(2,1)} %v_ref.1) | copy-start | bytes 25165828
  2.2 25.2 %copy-start.4 = (s32[8]{0:T(128)S(1)}, s32[8]{0:T(128)}, u32[]{:S(2)}) copy-start(s32[8]{0:T(128)} %len_ref.1) | copy-start | bytes 100
  36.4 0.6 copy-start.3

commit v3 on v2

--- a/solution.py
+++ b/solution.py
@@ -12,7 +12,7 @@
 BF = jnp.bfloat16
 F32 = jnp.float32
 MIB = 1024 * 1024
-UNROLL = 2
+UNROLL = 4
 
 
 def at(z, x):
@@ -24,7 +24,7 @@
                                         device_id=at(z, x), device_id_type=MESH)
 
 
-def group_barrier(z, x):
+def group_barrier(z, x, between=None):
     sem = pltpu.get_barrier_semaphore()
     me = z * 4 + x
 
@@ -34,6 +34,8 @@
         return c
 
     lax.fori_loop(1, 16, body, 0)
+    if between is not None:
+        between()
     pl.semaphore_wait(sem, 15)
 
 
@@ -71,8 +73,7 @@
         for zt, xt in late:
             arrived(slot(zt, xt))
         if consume is not None:
-            s0, s1 = slot(*first), slot(*second)
-            lax.fori_loop(0, 2, lambda i, c: (consume(s0 + i * (s1 - s0)), c)[1], 0)
+            consume(slot(*first), slot(*second))
 
     send(src_for(z), me, z, yx)
     for zt in near:
@@ -132,13 +133,12 @@
     return jnp.transpose(jnp.broadcast_to(r, (128, 128)))[:, 0:1]
 
 
-def normed(hb, gain_ref, g, r):
+def normed(hb, gain, g, r):
     w = hb.shape[2]
-    gain = gain_ref[:, pl.ds(pl.multiple_of(g * w, w), w)].astype(F32)
-    return (hb[g].astype(F32) * r * gain).astype(BF)
-
-
-def qkv_kernel(h_ref, gain_ref, w_hbm, out_ref, hb, wbuf, acc, scale, stat, zloc, zbuf,
+    return (hb[g].astype(F32) * r * gain[:, pl.ds(pl.multiple_of(g * w, w), w)].astype(F32)).astype(BF)
+
+
+def qkv_kernel(h_hbm, gain_hbm, w_hbm, out_ref, h_ref, gain, hb, wbuf, acc, scale, stat, zloc, zbuf,
                wsem, ssem, rsem, ssem_s, rsem_s, ssem2, rsem2):
     z, x = lax.axis_index("yz"), lax.axis_index("x")
     me = z * 4 + x
@@ -146,12 +146,15 @@
         pltpu.make_async_copy(w_hbm.at[0, pl.ds(pl.multiple_of(x * 256, 256), 256), :], wbuf.at[pl.ds(0, 256), :], wsem.at[0]),
         pltpu.make_async_copy(w_hbm.at[0, pl.ds(1024, 64), :], wbuf.at[pl.ds(256, 64), :], wsem.at[1]),
         pltpu.make_async_copy(w_hbm.at[0, pl.ds(1024, 64), :], wbuf.at[pl.ds(320, 64), :], wsem.at[2]),
+        pltpu.make_async_copy(gain_hbm, gain, wsem.at[3]),
     ]
+    mine = pltpu.make_async_copy(h_hbm, h_ref, wsem.at[4])
+    mine.start()
     for cp in parts:
         cp.start()
+    acc[...] = jnp.zeros_like(acc)
+    group_barrier(z, x, mine.wait)
     hb[x * 4 + z] = h_ref[...]
-    acc[...] = jnp.zeros_like(acc)
-    group_barrier(z, x)
     peer_s = share_sums(h_ref[...], stat, ssem_s, rsem_s, z, x)
 
     def ready():
@@ -159,9 +162,9 @@
         for cp in parts:
             cp.wait()
 
-    def consume(g):
-        u = normed(hb, gain_ref, g, scale[...])
-        w = wbuf[:, pl.ds(pl.multiple_of(g * 256, 256), 256)]
+    def consume(*pair):
+        u = jnp.concatenate([normed(hb, gain, g, scale[...]) for g in pair], axis=1)
+        w = jnp.concatenate([wbuf[:, pl.ds(pl.multiple_of(g * 256, 256), 256)] for g in pair], axis=1)
         acc[...] += lax.dot_general(u, w, (((1,), (1,)), ((), ())), preferred_element_type=F32)
 
     sent = gather(hb, lambda zt, xt: xt * 4 + zt, lambda zt: h_ref, ssem, rsem, z, x, ready, consume)
@@ -250,38 +253,42 @@
         p_new = (e_new * inv).astype(BF).astype(F32)
         orow[b] = jnp.dot(p, v_ref[0, b], preferred_element_type=F32) + p_new * v_new
 
+    def fix(b):
+        for which in range(2):
+            store(b, which).wait()
+            patch(b, which).start()
+
     def body(i, c):
         for k in range(UNROLL):
             one(i * UNROLL + k)
+        for k in range(UNROLL):
+            fix(i * UNROLL + k)
         return c
 
     lax.fori_loop(0, rows // UNROLL, body, 0)
     for h in range(heads):
         o_ref[h // 8, h % 8] = orow[:, h, :].astype(BF)
 
-    def fix(b, c):
-        for which in range(2):
-            store(b, which).wait()
-            patch(b, which).start()
-        return c
-
     def finish(b, c):
         for which in range(2):
             patch(b, which).wait()
         return c
 
-    lax.fori_loop(0, rows, fix, 0)
     lax.fori_loop(0, rows, finish, 0)
 
 
-def mlp_kernel(o_ref, h_ref, gain_ref, wo_hbm, wg_hbm, wd_hbm, out_ref,
-               wo, wg, wd, spread, obuf, olhs, part, recv, hb, acc, scale, stat, mbuf, part2, recv2,
+def mlp_kernel(o_hbm, h_hbm, gain_hbm, wo_hbm, wg_hbm, wd_hbm, out_ref,
+               o_ref, h_ref, gain, wo, wg, wd, spread, obuf, olhs, part, recv, hb, acc, scale, stat, mbuf, part2, recv2, total2,
                wsem, ssem_s, rsem_s, ssem_o, rsem_o, ssem_p, rsem_p, ssem_h, rsem_h, ssem_m, rsem_m, ssem_q, rsem_q):
     z, x = lax.axis_index("yz"), lax.axis_index("x")
     cols = pl.ds(pl.multiple_of(x * 1024, 1024), 1024)
     tiles = wg.shape[0]
     depth = wg.shape[1]
     flat = wg_hbm.at[0].reshape(depth, wg_hbm.shape[3])
+    small = [pltpu.make_async_copy(o_hbm, o_ref, wsem.at[2 + tiles]), pltpu.make_async_copy(h_hbm, h_ref, wsem.at[3 + tiles]),
+             pltpu.make_async_copy(gain_hbm, gain, wsem.at[4 + tiles])]
+    for cp in small:
+        cp.start()
     loads = [pltpu.make_async_copy(wo_hbm.at[0, :, cols], wo, wsem.at[0])]
     for j in range(tiles):
         lanes = pl.ds(pl.multiple_of((x * tiles + j) * 128, 128), 128)
@@ -289,88 +296,131 @@
     loads.append(pltpu.make_async_copy(wd_hbm.at[0, :, cols], wd, wsem.at[1 + tiles]))
     for cp in loads:
         cp.start()
-    group_barrier(z, x)
-
     k_id = lax.broadcasted_iota(jnp.int32, (256, 512), 0)
     c_id = lax.broadcasted_iota(jnp.int32, (256, 512), 1)
     spread[0] = jnp.where(c_id == 2 * k_id, 1.0, 0.0).astype(BF)
     spread[1] = jnp.where(c_id == 2 * k_id + 1, 1.0, 0.0).astype(BF)
-
-    obuf[z * 4 + x] = o_ref[z]
-    sent = gather(obuf, lambda zt, xt: zt * 4 + xt, lambda zt: o_ref.at[zt], ssem_o, rsem_o, z, x)
+    acc[...] = jnp.zeros_like(acc)
+
+    def settle():
+        for cp in small:
+            cp.wait()
+
+    group_barrier(z, x, settle)
+    yx = lax.rem(x + 2, 4)
+    cx = x + 1 - 2 * lax.rem(x, 2)
+    cyx = lax.rem(cx + 2, 4)
+    near = by_distance(z)
+
+    sent = []
+    mine = z * 4 + x
+    places = [(z, yx)] + [(zt, xt) for zt in near for xt in (x, yx)]
+
+    def o_send(src, s, zt, xt):
+        cp = remote(src, obuf.at[s], ssem_o.at[len(sent)], rsem_o.at[s], zt, xt)
+        cp.start()
+        sent.append(cp)
+
+    def o_arrived(zt, xt):
+        s = zt * 4 + xt
+        remote(obuf.at[s], obuf.at[s], ssem_o.at[0], rsem_o.at[s], z, x).wait_recv()
+
+    for zt, xt in places:
+        o_send(o_ref.at[zt], mine, zt, xt)
+    o_send(o_ref.at[z], mine, z, cx)
+    obuf[mine] = o_ref[z]
+    for zt, xt in places:
+        o_arrived(zt, xt)
+        o_send(obuf.at[zt * 4 + xt], zt * 4 + xt, z, cx)
+    for zt in (z, *near):
+        o_arrived(zt, cx)
+        o_arrived(zt, cyx)
     for h in range(8):
         olhs[:, h * 128:(h + 1) * 128] = obuf[:, h].reshape(128, 128)
 
-    def reduce_scatter(product, part, recv, ssem, rsem):
-        copies = []
-        for i, zt in enumerate(by_distance(z)):
-            part[zt] = product(zt).astype(BF)
-            cp = remote(part.at[zt], recv.at[z], ssem.at[i], rsem.at[z], zt, x)
-            cp.start()
-            copies.append(cp)
-        total = product(z)
-        for zt in by_distance(z):
-            remote(recv.at[zt], recv.at[zt], ssem.at[0], rsem.at[zt], z, x).wait_recv()
-            total += recv[zt].astype(F32)
-        return total, copies
-
     loads[0].wait()
 
     def out_block(zt):
         return jnp.dot(olhs[...], wo[:, pl.ds(pl.multiple_of(zt * 256, 256), 256)], preferred_element_type=F32)
 
-    total, more = reduce_scatter(out_block, part, recv, ssem_p, rsem_p)
-    sent += more
+    for i, zt in enumerate(near):
+        part[zt] = out_block(zt).astype(BF)
+        cp = remote(part.at[zt], recv.at[z], ssem_p.at[i], rsem_p.at[z], zt, x)
+        cp.start()
+        sent.append(cp)
+    total = out_block(z)
+    for zt in near:
+        remote(recv.at[zt], recv.at[zt], ssem_p.at[0], rsem_p.at[zt], z, x).wait_recv()
+        total += recv[zt].astype(F32)
     own = x * 4 + z
     hb[own] = (h_ref[...].astype(F32) + total).astype(BF)
     peer_s = share_sums(hb[own], stat, ssem_s, rsem_s, z, x)
-    acc[...] = jnp.zeros_like(acc)
 
     def ready():
         scale[...] = scale_of(stat, peer_s, ssem_s, rsem_s, z, x, 4096)
         for j in range(tiles):
             loads[1 + j].wait()
 
-    def consume(g):
-        u = normed(hb, gain_ref, g, scale[...])
-        even = jnp.dot(u, spread[0], preferred_element_type=F32).astype(BF)
-        odd = jnp.dot(u, spread[1], preferred_element_type=F32).astype(BF)
-        lhs = jnp.concatenate([even, odd], axis=0)
-        rows = pl.ds(pl.multiple_of(g * 512, 512), 512)
+    def consume(*pair):
+        lhs = []
+        for g in pair:
+            u = normed(hb, gain, g, scale[...])
+            even = jnp.dot(u, spread[0], preferred_element_type=F32).astype(BF)
+            odd = jnp.dot(u, spread[1], preferred_element_type=F32).astype(BF)
+            lhs.append(jnp.concatenate([even, odd], axis=0))
+        lhs = jnp.concatenate(lhs, axis=1)
         for j in range(0, tiles, 2):
             width = min(2, tiles - j)
-            w = jnp.concatenate([wg[j + i, rows, :] for i in range(width)], axis=1)
+            w = jnp.concatenate([
+                jnp.concatenate([wg[j + i, pl.ds(pl.multiple_of(g * 512, 512), 512), :] for i in range(width)], axis=1)
+                for g in pair], axis=0)
             acc[:, j * 128:(j + width) * 128] += jnp.dot(lhs, w, preferred_element_type=F32)
 
     sent += gather(hb, lambda zt, xt: xt * 4 + zt, lambda zt: hb.at[own], ssem_h, rsem_h, z, x, ready, consume)
     gate = acc[0:128, :].astype(BF).astype(F32)
     up = acc[128:256, :].astype(BF).astype(F32)
-    mbuf[x] = (jax.nn.silu(gate) * up).astype(BF)
-
-    yx = lax.rem(x + 2, 4)
-    cx = x + 1 - 2 * lax.rem(x, 2)
-    cyx = lax.rem(cx + 2, 4)
-    mcopies = [remote(mbuf.at[x], mbuf.at[x], ssem_m.at[0], rsem_m.at[x], z, yx),
-               remote(mbuf.at[x], mbuf.at[x], ssem_m.at[1], rsem_m.at[x], z, cx)]
-    for cp in mcopies:
-        cp.start()
-    remote(mbuf.at[yx], mbuf.at[yx], ssem_m.at[0], rsem_m.at[yx], z, x).wait_recv()
-    cp = remote(mbuf.at[yx], mbuf.at[yx], ssem_m.at[2], rsem_m.at[yx], z, cx)
-    cp.start()
-    sent += mcopies + [cp]
-    for xt in (cx, cyx):
-        remote(mbuf.at[xt], mbuf.at[xt], ssem_m.at[0], rsem_m.at[xt], z, x).wait_recv()
+    m = (jax.nn.silu(gate) * up).astype(BF)
+    halves, half = mbuf.shape[0], mbuf.shape[2]
+    for f in range(halves):
+        mbuf[f, x] = m[f * half:(f + 1) * half, :]
+
+    def m_send(f, xt, target, i):
+        cp = remote(mbuf.at[f, xt], mbuf.at[f, xt], ssem_m.at[f, i], rsem_m.at[f, xt], z, target)
+        cp.start()
+        sent.append(cp)
+
+    def m_arrived(f, xt):
+        remote(mbuf.at[f, xt], mbuf.at[f, xt], ssem_m.at[f, 0], rsem_m.at[f, xt], z, x).wait_recv()
+
+    for f in range(halves):
+        m_send(f, x, yx, 0)
+        m_send(f, x, cx, 1)
     loads[1 + tiles].wait()
 
-    def down_block(zt):
+    def down_block(f, zt):
         lanes = pl.ds(pl.multiple_of(zt * 256, 256), 256)
-        width = mbuf.shape[2]
+        width = mbuf.shape[3]
         return functools.reduce(lambda a, b: a + b, [
-            jnp.dot(mbuf[i], wd[i * width:(i + 1) * width, lanes], preferred_element_type=F32) for i in range(4)])
-
-    total, more = reduce_scatter(down_block, part2, recv2, ssem_q, rsem_q)
-    sent += more
-    out_ref[...] = (hb[own].astype(F32) + total).astype(BF)
+            jnp.dot(mbuf[f, i], wd[i * width:(i + 1) * width, lanes], preferred_element_type=F32) for i in range(4)])
+
+    for f in range(halves):
+        m_arrived(f, yx)
+        m_send(f, yx, cx, 2)
+        m_arrived(f, cx)
+        m_arrived(f, cyx)
+        for i, zt in enumerate(near):
+            part2[f, zt] = down_block(f, zt).astype(BF)
+            cp = remote(part2.at[f, zt], recv2.at[f, z], ssem_q.at[f, i], rsem_q.at[f, z], zt, x)
+            cp.start()
+            sent.append(cp)
+        total2[f] = down_block(f, z)
+    for f in range(halves):
+        total = total2[f]
+        for zt in near:
+            remote(recv2.at[f, zt], recv2.at[f, zt], ssem_q.at[f, 0], rsem_q.at[f, zt], z, x).wait_recv()
+            total += recv2[f, zt].astype(F32)
+        rows = slice(f * half, (f + 1) * half)
+        out_ref[rows, :] = (hb[own, rows, :].astype(F32) + total).astype(BF)
     for cp in sent:
         cp.wait_send()
 
@@ -389,12 +439,12 @@
         z_rows = pl.pallas_call(
             qkv_kernel,
             out_shape=sd((16, 8, 384), BF),
-            in_specs=[vmem, vmem, hbm],
+            in_specs=[hbm, hbm, hbm],
             out_specs=vmem,
-            scratch_shapes=[pltpu.VMEM((16, 128, 256), BF), pltpu.VMEM((384, 4096), BF), pltpu.VMEM((128, 384), F32),
+            scratch_shapes=[pltpu.VMEM((128, 256), BF), pltpu.VMEM((1, 4096), BF), pltpu.VMEM((16, 128, 256), BF), pltpu.VMEM((384, 4096), BF), pltpu.VMEM((128, 384), F32),
                             pltpu.VMEM((128, 1), F32), pltpu.VMEM((16, 1, 128), F32),
                             pltpu.VMEM((16, 8, 384), BF), pltpu.VMEM((16, 8, 384), BF),
-                            dma((3,)), dma((15,)), dma((16,)), dma((16,)), dma((16,)), dma((16,)), dma((16,))],
+                            dma((5,)), dma((15,)), dma((16,)), dma((16,)), dma((16,)), dma((16,)), dma((16,))],
             compiler_params=pltpu.CompilerParams(collective_id=0, has_side_effects=True, vmem_limit_bytes=46 * MIB),
             cost_estimate=pl.CostEstimate(flops=30_000_000_000, bytes_accessed=20_000_000, transcendentals=0),
             name="qkv",
@@ -413,16 +463,17 @@
         hidden = pl.pallas_call(
             mlp_kernel,
             out_shape=sd(hidden.shape, BF),
-            in_specs=[vmem, vmem, vmem, hbm, hbm, hbm],
+            in_specs=[hbm] * 6,
             out_specs=vmem,
-            scratch_shapes=[pltpu.VMEM((1024, 1024), BF), pltpu.VMEM((7, 8192, 128), BF), pltpu.VMEM((3584, 1024), BF),
+            scratch_shapes=[pltpu.VMEM((4, 8, 8, 128), BF), pltpu.VMEM((128, 256), BF), pltpu.VMEM((1, 4096), BF),
+                            pltpu.VMEM((1024, 1024), BF), pltpu.VMEM((7, 8192, 128), BF), pltpu.VMEM((3584, 1024), BF),
                             pltpu.VMEM((2, 256, 512), BF), pltpu.VMEM((16, 8, 8, 128), BF), pltpu.VMEM((128, 1024), BF),
                             pltpu.VMEM((4, 128, 256), BF), pltpu.VMEM((4, 128, 256), BF), pltpu.VMEM((16, 128, 256), BF),
                             pltpu.VMEM((256, 896), F32), pltpu.VMEM((128, 1), F32), pltpu.VMEM((16, 1, 128), F32),
-                            pltpu.VMEM((4, 128, 896), BF),
-                            pltpu.VMEM((4, 128, 256), BF), pltpu.VMEM((4, 128, 256), BF),
-                            dma((9,)), dma((16,)), dma((16,)), dma((15,)), dma((16,)), dma((3,)), dma((4,)), dma((15,)), dma((16,)),
-                            dma((3,)), dma((4,)), dma((3,)), dma((4,))],
+                            pltpu.VMEM((2, 4, 64, 896), BF),
+                            pltpu.VMEM((2, 4, 64, 256), BF), pltpu.VMEM((2, 4, 64, 256), BF), pltpu.VMEM((2, 64, 256), F32),
+                            dma((12,)), dma((16,)), dma((16,)), dma((15,)), dma((16,)), dma((3,)), dma((4,)), dma((15,)), dma((16,)),
+                            dma((2, 3)), dma((2, 4)), dma((2, 3)), dma((2, 4))],
             compiler_params=pltpu.CompilerParams(collective_id=1, has_side_effects=True, vmem_limit_bytes=56 * MIB),
             name="mlp",
         )(o, hidden, mlp_gain, w_out, w_gate_up, w_down)

time: 91 us -> 85.1 us (0.935)
  Pallas kernels: 86.4 us -> 80.5 us
    pallas_call x2, Pallas kernels: 77.4 us -> 71.8 us  [the longest x1 46.9 us: layer(): pl.pallas_call(mlp_kernel, out_shape=sd(hidden.shape, BF), in_specs=[hbm]...]
where the time goes in v3:
time: 85.1 us; the launch traced here: 84.8 us
  Pallas kernels  80.5 us (95%)
  local copies, waits for them, and re-layouts  3.66 us (4%)
    pallas_call x1, Pallas kernels, layer(): pl.pallas_call(mlp_kernel, out_shape=sd(hidden.shape, BF), in_specs=[hbm]...  46.9 us
    pallas_call x1, Pallas kernels, layer(): pl.pallas_call(qkv_kernel, out_shape=sd((16, 8, 384), BF), in_specs=[hbm,...  24.9 us
    pallas_call x1, Pallas kernels, layer(): pl.pallas_call(attn_kernel, out_shape=(sd((4, 8, rows, hd), BF), sd(k_cac...  8.69 us
    unnamed x13, local copies, waits for them, and re-layouts  3.66 us

profile of v3, /device:TPU:0, one launch (start us, length us, event | category | flops | bytes accessed | tf_op | source)
XLA Modules:
  0.0 84.8 jit_solution(11230102673126714615)
XLA Ops:
  0.6 0.0 copy-start.2
  0.6 0.8 copy-done.2
  1.5 0.0 copy-start.5
  1.5 0.7 copy-done.5
  2.2 0.0 copy-start
  2.2 0.0 copy-start.1
  2.2 0.0 copy-start.4
  2.2 24.9 %qkv.1.z_ref = bf16[16,8,384]{2,1,0:T(8,128)(2,1)S(1)} custom-call(bf16[128,256]{1,0:T(8,128)(2,1)S(1)} %copy-done.2, bf16[1,4096]{1,0:T(2,128)(2,1)S(1)} %copy-done.5, bf16[1,1088,4096]{2,1,0:T(8,128)(2,1)} %bitcast.1), custom_call_target="tpu_custom_call" | custom-call | flops 30000001024 | bytes 20000000 | tf_op jit(solution)/shard_map/qkv/pallas_call | solution.py:439
  27.1 0.0 copy-done
  27.1 0.0 copy-done.1
  27.1 0.0 copy-done.4
  27.1 8.7 %attend.1 = (bf16[4,8,8,128]{3,2,1,0:T(8,128)(2,1)S(1)}, bf16[1,8,4096,128]{3,2,1,0:T(8,128)(2,1)}, bf16[1,8,4096,128]{3,2,1,0:T(8,128)(2,1)}) custom-call(s32[8]{0:T(128)S(1)} %copy-done.4, bf16[16,8,384]{2,1,0:T(8,128)(2,1)S(1)} %qkv.1.z_ref, bf16[1,8,4096,128]{3,2,1,0:T(8,128)(2,1)S(1)} %copy-done, bf16[1,8,4096,128]{3,2,1,0:T(8,128)(2,1)S(1)} %copy-done.1), custom_call_target="tpu_custom_call" | custom-call | tf_op jit(solution)/shard_map/attend/pallas_call | solution.py:453
  35.8 0.0 copy-start.3
  35.8 0.6 copy-done.3
  36.5 46.9 %mlp.1 = bf16[128,256]{1,0:T(8,128)(2,1)} custom-call(bf16[4,8,8,128]{3,2,1,0:T(8,128)(2,1)} %copy-done.3, bf16[128,256]{1,0:T(8,128)(2,1)} %h_hbm.3, bf16[1,4096]{1,0:T(2,128)(2,1)} %gain_hbm.3, bf16[1,1024,4096]{2,1,0:T(8,128)(2,1)} %wo_hbm.1, bf16[1,4096,2,3584]{3,2,1,0:T(2,128)(2,1)} %wg_hbm.1, bf16[1,3584,4096]{2,1,0:T(8,128)(2,1)} %wd_hbm.1), custom_call_target="tpu_custom_call" | custom-call | tf_op jit(solution)/shard_map/mlp/pallas_call | solution.py:463
  83.4 1.5 %copy.14 = bf16[128,256]{1,0:T(8,128)(2,1)} copy(bf16[128,256]{1,0:T(8,128)(2,1)} %mlp.1) | data formatting | bytes 131072
Async XLA Ops:
  0.6 0.8 copy-start.2
  1.5 0.7 copy-start.5
  2.2 24.9 %copy-start = (bf16[1,8,4096,128]{3,2,1,0:T(8,128)(2,1)S(1)}, bf16[1,8,4096,128]{3,2,1,0:T(8,128)(2,1)}, u32[]{:S(2)}) copy-start(bf16[1,8,4096,128]{3,2,1,0:T(8,128)(2,1)} %k_ref.1) | copy-start | bytes 25165828
  2.2 24.9 %copy-start.1 = (bf16[1,8,4096,128]{3,2,1,0:T(8,128)(2,1)S(1)}, bf16[1,8,4096,128]{3,2,1,0:T(8,128)(2,1)}, u32[]{:S(2)}) copy-start(bf16[1,8,4096,128]{3,2,1,0:T(8,128)(2,1)} %v_ref.1) | copy-start | bytes 25165828
  2.2 24.9 %copy-start.4 = (s32[8]{0:T(128)S(1)}, s32[8]{0:T(128)}, u32[]{:S(2)}) copy-start(s32[8]{0:T(128)} %len_ref.1) | copy-start | bytes 100
  35.8 0.6 copy-start.3

commit v4 on v3

--- a/solution.py
+++ b/solution.py
@@ -12,7 +12,7 @@
 BF = jnp.bfloat16
 F32 = jnp.float32
 MIB = 1024 * 1024
-UNROLL = 4
+UNROLL = 2
 
 
 def at(z, x):
@@ -47,7 +47,7 @@
     return n1, n2, 6 - z - n1 - n2
 
 
-def gather(buf, slot, src_for, ssem, rsem, z, x, ready=None, consume=None):
+def gather(buf, slot, src_for, ssem, rsem, z, x, sent_own, ready, consume):
     yx = lax.rem(x + 2, 4)
     cx = x + 1 - 2 * lax.rem(x, 2)
     cyx = lax.rem(cx + 2, 4)
@@ -72,17 +72,16 @@
     def work(first, second, *late):
         for zt, xt in late:
             arrived(slot(zt, xt))
-        if consume is not None:
-            consume(slot(*first), slot(*second))
-
+        consume(slot(*first), slot(*second))
+
+    for zt in reversed(near):
+        send(src_for(zt), me, zt, x)
     send(src_for(z), me, z, yx)
-    for zt in near:
-        send(src_for(zt), me, zt, x)
     send(src_for(z), me, z, cx)
+    sent_own()
     pass_on(z, yx, cx)
     pass_on(n1, x, yx, cx)
-    if ready is not None:
-        ready()
+    ready()
     work((z, x), (z, yx))
     pass_on(n2, x, yx, cx)
     work((n1, x), (z, cx), (z, cx))
@@ -115,14 +114,13 @@
         return c
 
     lax.fori_loop(1, 16, start, 0)
-    return peer
-
-
-def scale_of(stat, peer, ssem, rsem, z, x, width):
+
+
+def scale_of(stat, ssem, rsem, z, x, width):
     me = z * 4 + x
 
     def finish(p, c):
-        peer(p).wait_send()
+        remote(stat.at[me], stat.at[me], ssem.at[p], rsem.at[me], z, x).wait_send()
         d = lax.rem(me + p, 16)
         remote(stat.at[d], stat.at[d], ssem.at[0], rsem.at[d], z, x).wait_recv()
         return c
@@ -154,11 +152,13 @@
         cp.start()
     acc[...] = jnp.zeros_like(acc)
     group_barrier(z, x, mine.wait)
-    hb[x * 4 + z] = h_ref[...]
-    peer_s = share_sums(h_ref[...], stat, ssem_s, rsem_s, z, x)
+
+    def sent_own():
+        share_sums(h_ref[...], stat, ssem_s, rsem_s, z, x)
+        hb[x * 4 + z] = h_ref[...]
 
     def ready():
-        scale[...] = scale_of(stat, peer_s, ssem_s, rsem_s, z, x, 4096)
+        scale[...] = scale_of(stat, ssem_s, rsem_s, z, x, 4096)
         for cp in parts:
             cp.wait()
 
@@ -167,7 +167,7 @@
         w = jnp.concatenate([wbuf[:, pl.ds(pl.multiple_of(g * 256, 256), 256)] for g in pair], axis=1)
         acc[...] += lax.dot_general(u, w, (((1,), (1,)), ((), ())), preferred_element_type=F32)
 
-    sent = gather(hb, lambda zt, xt: xt * 4 + zt, lambda zt: h_ref, ssem, rsem, z, x, ready, consume)
+    sent = gather(hb, lambda zt, xt: xt * 4 + zt, lambda zt: h_ref, ssem, rsem, z, x, sent_own, ready, consume)
     for d in range(16):
         zloc[d] = acc[d * 8:(d + 1) * 8, :].astype(BF)
 
@@ -235,11 +235,16 @@
         hit = lax.broadcasted_iota(jnp.int32, (16, hd), 0) == pos - lo
         return jnp.where(hit, row, tile).astype(BF)
 
+    def renew(b, c):
+        tiles[0, b] = updated(k_ref, b, zrow[b, heads:heads + 1, :], len_ref[b])
+        tiles[1, b] = updated(v_ref, b, zrow[b, heads + 1:heads + 2, :], len_ref[b])
+        return c
+
+    lax.fori_loop(0, rows, renew, 0)
+
     def one(b):
         pos = len_ref[b]
         k_new, v_new = zrow[b, heads:heads + 1, :], zrow[b, heads + 1:heads + 2, :]
-        tiles[0, b] = updated(k_ref, b, k_new, pos)
-        tiles[1, b] = updated(v_ref, b, v_new, pos)
         q = zrow[b, 0:heads, :]
         s = lax.dot_general(q.astype(BF), k_ref[0, b], (((1,), (1,)), ((), ())), preferred_element_type=F32)
         s_new = jnp.sum(q * k_new, axis=1, keepdims=True)
@@ -261,11 +266,17 @@
     def body(i, c):
         for k in range(UNROLL):
             one(i * UNROLL + k)
-        for k in range(UNROLL):
-            fix(i * UNROLL + k)
-        return c
-
-    lax.fori_loop(0, rows // UNROLL, body, 0)
+        return c
+
+    def patches(b, c):
+        fix(b)
+        return c
+
+    lax.fori_loop(0, rows // UNROLL - 1, body, 0)
+    for b in range(rows - UNROLL, rows - 1):
+        one(b)
+    lax.fori_loop(0, rows, patches, 0)
+    one(rows - 1)
     for h in range(heads):
         o_ref[h // 8, h % 8] = orow[:, h, :].astype(BF)
 
@@ -325,7 +336,7 @@
         s = zt * 4 + xt
         remote(obuf.at[s], obuf.at[s], ssem_o.at[0], rsem_o.at[s], z, x).wait_recv()
 
-    for zt, xt in places:
+    for zt, xt in reversed(places):
         o_send(o_ref.at[zt], mine, zt, xt)
     o_send(o_ref.at[z], mine, z, cx)
     obuf[mine] = o_ref[z]
@@ -343,7 +354,7 @@
     def out_block(zt):
         return jnp.dot(olhs[...], wo[:, pl.ds(pl.multiple_of(zt * 256, 256), 256)], preferred_element_type=F32)
 
-    for i, zt in enumerate(near):
+    for i, zt in enumerate(reversed(near)):
         part[zt] = out_block(zt).astype(BF)
         cp = remote(part.at[zt], recv.at[z], ssem_p.at[i], rsem_p.at[z], zt, x)
         cp.start()
@@ -354,10 +365,12 @@
         total += recv[zt].astype(F32)
     own = x * 4 + z
     hb[own] = (h_ref[...].astype(F32) + total).astype(BF)
-    peer_s = share_sums(hb[own], stat, ssem_s, rsem_s, z, x)
+
+    def sent_own():
+        share_sums(hb[own], stat, ssem_s, rsem_s, z, x)
 
     def ready():
-        scale[...] = scale_of(stat, peer_s, ssem_s, rsem_s, z, x, 4096)
+        scale[...] = scale_of(stat, ssem_s, rsem_s, z, x, 4096)
         for j in range(tiles):
             loads[1 + j].wait()
 
@@ -376,13 +389,8 @@
                 for g in pair], axis=0)
             acc[:, j * 128:(j + width) * 128] += jnp.dot(lhs, w, preferred_element_type=F32)
 
-    sent += gather(hb, lambda zt, xt: xt * 4 + zt, lambda zt: hb.at[own], ssem_h, rsem_h, z, x, ready, consume)
-    gate = acc[0:128, :].astype(BF).astype(F32)
-    up = acc[128:256, :].astype(BF).astype(F32)
-    m = (jax.nn.silu(gate) * up).astype(BF)
+    sent += gather(hb, lambda zt, xt: xt * 4 + zt, lambda zt: hb.at[own], ssem_h, rsem_h, z, x, sent_own, ready, consume)
     halves, half = mbuf.shape[0], mbuf.shape[2]
-    for f in range(halves):
-        mbuf[f, x] = m[f * half:(f + 1) * half, :]
 
     def m_send(f, xt, target, i):
         cp = remote(mbuf.at[f, xt], mbuf.at[f, xt], ssem_m.at[f, i], rsem_m.at[f, xt], z, target)
@@ -393,6 +401,9 @@
         remote(mbuf.at[f, xt], mbuf.at[f, xt], ssem_m.at[f, 0], rsem_m.at[f, xt], z, x).wait_recv()
 
     for f in range(halves):
+        gate = acc[f * half:(f + 1) * half, :].astype(BF).astype(F32)
+        up = acc[128 + f * half:128 + (f + 1) * half, :].astype(BF).astype(F32)
+        mbuf[f, x] = (jax.nn.silu(gate) * up).astype(BF)
         m_send(f, x, yx, 0)
         m_send(f, x, cx, 1)
     loads[1 + tiles].wait()
@@ -408,7 +419,7 @@
         m_send(f, yx, cx, 2)
         m_arrived(f, cx)
         m_arrived(f, cyx)
-        for i, zt in enumerate(near):
+        for i, zt in enumerate(reversed(near)):
             part2[f, zt] = down_block(f, zt).astype(BF)
             cp = remote(part2.at[f, zt], recv2.at[f, z], ssem_q.at[f, i], rsem_q.at[f, z], zt, x)
             cp.start()
@@ -474,7 +485,7 @@
                             pltpu.VMEM((2, 4, 64, 256), BF), pltpu.VMEM((2, 4, 64, 256), BF), pltpu.VMEM((2, 64, 256), F32),
                             dma((12,)), dma((16,)), dma((16,)), dma((15,)), dma((16,)), dma((3,)), dma((4,)), dma((15,)), dma((16,)),
                             dma((2, 3)), dma((2, 4)), dma((2, 3)), dma((2, 4))],
-            compiler_params=pltpu.CompilerParams(collective_id=1, has_side_effects=True, vmem_limit_bytes=56 * MIB),
+            compiler_params=pltpu.CompilerParams(collective_id=1, has_side_effects=True, vmem_limit_bytes=48 * MIB),
             name="mlp",
         )(o, hidden, mlp_gain, w_out, w_gate_up, w_down)
         return hidden, k_out, v_out

time: 85.1 us -> 86.9 us (1.021)
  Pallas kernels: 80.5 us -> 83.7 us
  local copies, waits for them, and re-layouts: 3.66 us -> 2.21 us
    pallas_call x1, Pallas kernels: 46.9 us -> 49.7 us  [layer(): pl.pallas_call(mlp_kernel, out_shape=sd(hidden.shape, BF), in_specs=[hbm]...]
    unnamed x13 -> x15, local copies, waits for them, and re-layouts: 3.66 us -> 2.21 us
where the time goes in v4:
time: 86.9 us; the launch traced here: 86.6 us
  Pallas kernels  83.7 us (96%)
  local copies, waits for them, and re-layouts  2.21 us (3%)
    pallas_call x1, Pallas kernels, layer(): pl.pallas_call(mlp_kernel, out_shape=sd(hidden.shape, BF), in_specs=[hbm]...  49.7 us
    pallas_call x1, Pallas kernels, layer(): pl.pallas_call(qkv_kernel, out_shape=sd((16, 8, 384), BF), in_specs=[hbm,...  25.4 us
    pallas_call x1, Pallas kernels, layer(): pl.pallas_call(attn_kernel, out_shape=(sd((4, 8, rows, hd), BF), sd(k_cac...  8.57 us
    unnamed x15, local copies, waits for them, and re-layouts  2.21 us

profile of v4, /device:TPU:0, one launch (start us, length us, event | category | flops | bytes accessed | tf_op | source)
XLA Modules:
  0.0 86.6 jit_solution(8996277576823791855)
XLA Ops:
  0.6 0.0 copy-start.2
  0.6 0.8 copy-done.2
  1.5 0.0 copy-start.6
  1.5 0.7 copy-done.6
  2.2 0.0 copy-start
  2.2 0.0 copy-start.1
  2.2 0.0 copy-start.5
  2.2 25.4 %qkv.1.z_ref = bf16[16,8,384]{2,1,0:T(8,128)(2,1)S(1)} custom-call(bf16[128,256]{1,0:T(8,128)(2,1)S(1)} %copy-done.2, bf16[1,4096]{1,0:T(2,128)(2,1)S(1)} %copy-done.6, bf16[1,1088,4096]{2,1,0:T(8,128)(2,1)} %bitcast.1), custom_call_target="tpu_custom_call" | custom-call | flops 30000001024 | bytes 20000000 | tf_op jit(solution)/shard_map/qkv/pallas_call | solution.py:450
  27.6 0.0 copy-done
  27.7 0.0 copy-done.1
  27.7 0.0 copy-done.5
  27.7 0.0 copy-start.3
  27.7 0.0 copy-start.4
  27.7 8.6 %attend.1 = (bf16[4,8,8,128]{3,2,1,0:T(8,128)(2,1)S(1)}, bf16[1,8,4096,128]{3,2,1,0:T(8,128)(2,1)}, bf16[1,8,4096,128]{3,2,1,0:T(8,128)(2,1)}) custom-call(s32[8]{0:T(128)S(1)} %copy-done.5, bf16[16,8,384]{2,1,0:T(8,128)(2,1)S(1)} %qkv.1.z_ref, bf16[1,8,4096,128]{3,2,1,0:T(8,128)(2,1)S(1)} %copy-done, bf16[1,8,4096,128]{3,2,1,0:T(8,128)(2,1)S(1)} %copy-done.1), custom_call_target="tpu_custom_call" | custom-call | tf_op jit(solution)/shard_map/attend/pallas_call | solution.py:464
  36.3 0.0 copy-done.3
  36.3 0.0 copy-done.4
  36.3 49.7 %mlp.1 = bf16[128,256]{1,0:T(8,128)(2,1)S(1)} custom-call(bf16[4,8,8,128]{3,2,1,0:T(8,128)(2,1)S(1)} %get-tuple-element.6.o_hbm, bf16[128,256]{1,0:T(8,128)(2,1)S(1)} %copy-done.3, bf16[1,4096]{1,0:T(2,128)(2,1)S(1)} %copy-done.4, bf16[1,1024,4096]{2,1,0:T(8,128)(2,1)} %wo_hbm.1, bf16[1,4096,2,3584]{3,2,1,0:T(2,128)(2,1)} %wg_hbm.1, ...), custom_call_target="tpu_custom_call" | custom-call | tf_op jit(solution)/shard_map/mlp/pallas_call | solution.py:474
  86.0 0.6 copy.14
Async XLA Ops:
  0.6 0.8 copy-start.2
  1.5 0.7 copy-start.6
  2.2 25.5 %copy-start = (bf16[1,8,4096,128]{3,2,1,0:T(8,128)(2,1)S(1)}, bf16[1,8,4096,128]{3,2,1,0:T(8,128)(2,1)}, u32[]{:S(2)}) copy-start(bf16[1,8,4096,128]{3,2,1,0:T(8,128)(2,1)} %k_ref.1) | copy-start | bytes 25165828
  2.2 25.5 %copy-start.1 = (bf16[1,8,4096,128]{3,2,1,0:T(8,128)(2,1)S(1)}, bf16[1,8,4096,128]{3,2,1,0:T(8,128)(2,1)}, u32[]{:S(2)}) copy-start(bf16[1,8,4096,128]{3,2,1,0:T(8,128)(2,1)} %v_ref.1) | copy-start | bytes 25165828
  2.2 25.5 %copy-start.5 = (s32[8]{0:T(128)S(1)}, s32[8]{0:T(128)}, u32[]{:S(2)}) copy-start(s32[8]{0:T(128)} %len_ref.1) | copy-start | bytes 100
  27.7 8.6 %copy-start.3 = (bf16[128,256]{1,0:T(8,128)(2,1)S(1)}, bf16[128,256]{1,0:T(8,128)(2,1)}, u32[]{:S(2)}) copy-start(bf16[128,256]{1,0:T(8,128)(2,1)} %h_hbm.3) | copy-start | bytes 196612
  27.7 8.6 %copy-start.4 = (bf16[1,4096]{1,0:T(2,128)(2,1)S(1)}, bf16[1,4096]{1,0:T(2,128)(2,1)}, u32[]{:S(2)}) copy-start(bf16[1,4096]{1,0:T(2,128)(2,1)} %gain_hbm.3) | copy-start | bytes 24580

commit v5 on v4

--- a/solution.py
+++ b/solution.py
@@ -47,7 +47,7 @@
     return n1, n2, 6 - z - n1 - n2
 
 
-def gather(buf, slot, src_for, ssem, rsem, z, x, sent_own, ready, consume):
+def gather(buf, slot, src_for, ssem, rsem, z, x, ready, consume):
     yx = lax.rem(x + 2, 4)
     cx = x + 1 - 2 * lax.rem(x, 2)
     cyx = lax.rem(cx + 2, 4)
@@ -74,11 +74,10 @@
             arrived(slot(zt, xt))
         consume(slot(*first), slot(*second))
 
-    for zt in reversed(near):
+    send(src_for(z), me, z, yx)
+    for zt in near:
         send(src_for(zt), me, zt, x)
-    send(src_for(z), me, z, yx)
     send(src_for(z), me, z, cx)
-    sent_own()
     pass_on(z, yx, cx)
     pass_on(n1, x, yx, cx)
     ready()
@@ -152,10 +151,8 @@
         cp.start()
     acc[...] = jnp.zeros_like(acc)
     group_barrier(z, x, mine.wait)
-
-    def sent_own():
-        share_sums(h_ref[...], stat, ssem_s, rsem_s, z, x)
-        hb[x * 4 + z] = h_ref[...]
+    share_sums(h_ref[...], stat, ssem_s, rsem_s, z, x)
+    hb[x * 4 + z] = h_ref[...]
 
     def ready():
         scale[...] = scale_of(stat, ssem_s, rsem_s, z, x, 4096)
@@ -167,7 +164,7 @@
         w = jnp.concatenate([wbuf[:, pl.ds(pl.multiple_of(g * 256, 256), 256)] for g in pair], axis=1)
         acc[...] += lax.dot_general(u, w, (((1,), (1,)), ((), ())), preferred_element_type=F32)
 
-    sent = gather(hb, lambda zt, xt: xt * 4 + zt, lambda zt: h_ref, ssem, rsem, z, x, sent_own, ready, consume)
+    sent = gather(hb, lambda zt, xt: xt * 4 + zt, lambda zt: h_ref, ssem, rsem, z, x, ready, consume)
     for d in range(16):
         zloc[d] = acc[d * 8:(d + 1) * 8, :].astype(BF)
 
@@ -289,7 +286,7 @@
 
 
 def mlp_kernel(o_hbm, h_hbm, gain_hbm, wo_hbm, wg_hbm, wd_hbm, out_ref,
-               o_ref, h_ref, gain, wo, wg, wd, spread, obuf, olhs, part, recv, hb, acc, scale, stat, mbuf, part2, recv2, total2,
+               o_ref, h_ref, gain, wo, wg, wd, spread, obuf, olhs, part, recv, hb, acc, scale, stat, mbuf, low, part2, recv2,
                wsem, ssem_s, rsem_s, ssem_o, rsem_o, ssem_p, rsem_p, ssem_h, rsem_h, ssem_m, rsem_m, ssem_q, rsem_q):
     z, x = lax.axis_index("yz"), lax.axis_index("x")
     cols = pl.ds(pl.multiple_of(x * 1024, 1024), 1024)
@@ -307,10 +304,9 @@
     loads.append(pltpu.make_async_copy(wd_hbm.at[0, :, cols], wd, wsem.at[1 + tiles]))
     for cp in loads:
         cp.start()
-    k_id = lax.broadcasted_iota(jnp.int32, (256, 512), 0)
-    c_id = lax.broadcasted_iota(jnp.int32, (256, 512), 1)
-    spread[0] = jnp.where(c_id == 2 * k_id, 1.0, 0.0).astype(BF)
-    spread[1] = jnp.where(c_id == 2 * k_id + 1, 1.0, 0.0).astype(BF)
+    k_id = lax.broadcasted_iota(jnp.int32, (256, 1024), 0)
+    c_id = lax.broadcasted_iota(jnp.int32, (256, 1024), 1)
+    spread[...] = jnp.where(c_id == 2 * k_id + (c_id // 512) * 513, 1.0, 0.0).astype(BF)
     acc[...] = jnp.zeros_like(acc)
 
     def settle():
@@ -336,7 +332,7 @@
         s = zt * 4 + xt
         remote(obuf.at[s], obuf.at[s], ssem_o.at[0], rsem_o.at[s], z, x).wait_recv()
 
-    for zt, xt in reversed(places):
+    for zt, xt in places:
         o_send(o_ref.at[zt], mine, zt, xt)
     o_send(o_ref.at[z], mine, z, cx)
     obuf[mine] = o_ref[z]
@@ -351,23 +347,24 @@
 
     loads[0].wait()
 
-    def out_block(zt):
-        return jnp.dot(olhs[...], wo[:, pl.ds(pl.multiple_of(zt * 256, 256), 256)], preferred_element_type=F32)
-
-    for i, zt in enumerate(reversed(near)):
-        part[zt] = out_block(zt).astype(BF)
+    def block(zt):
+        return pl.ds(pl.multiple_of(zt * 256, 256), 256)
+
+    for n in range(4):
+        lanes = slice(n * 256, (n + 1) * 256)
+        low[:, lanes] = jnp.dot(olhs[...], wo[:, lanes], preferred_element_type=F32)
+    for i, zt in enumerate(near):
+        part[zt] = low[:, block(zt)].astype(BF)
         cp = remote(part.at[zt], recv.at[z], ssem_p.at[i], rsem_p.at[z], zt, x)
         cp.start()
         sent.append(cp)
-    total = out_block(z)
+    total = low[:, block(z)]
     for zt in near:
         remote(recv.at[zt], recv.at[zt], ssem_p.at[0], rsem_p.at[zt], z, x).wait_recv()
         total += recv[zt].astype(F32)
     own = x * 4 + z
     hb[own] = (h_ref[...].astype(F32) + total).astype(BF)
-
-    def sent_own():
-        share_sums(hb[own], stat, ssem_s, rsem_s, z, x)
+    share_sums(hb[own], stat, ssem_s, rsem_s, z, x)
 
     def ready():
         scale[...] = scale_of(stat, ssem_s, rsem_s, z, x, 4096)
@@ -375,12 +372,11 @@
             loads[1 + j].wait()
 
     def consume(*pair):
-        lhs = []
-        for g in pair:
-            u = normed(hb, gain, g, scale[...])
-            even = jnp.dot(u, spread[0], preferred_element_type=F32).astype(BF)
-            odd = jnp.dot(u, spread[1], preferred_element_type=F32).astype(BF)
-            lhs.append(jnp.concatenate([even, odd], axis=0))
+        u = jnp.concatenate([normed(hb, gain, g, scale[...]) for g in pair], axis=0)
+        wide = jnp.dot(u, spread[...], preferred_element_type=F32).astype(BF)
+        rows, width = hb.shape[1], wide.shape[1] // 2
+        lhs = [jnp.concatenate([wide[i * rows:(i + 1) * rows, :width], wide[i * rows:(i + 1) * rows, width:]], axis=0)
+               for i in range(len(pair))]
         lhs = jnp.concatenate(lhs, axis=1)
         for j in range(0, tiles, 2):
             width = min(2, tiles - j)
@@ -389,7 +385,7 @@
                 for g in pair], axis=0)
             acc[:, j * 128:(j + width) * 128] += jnp.dot(lhs, w, preferred_element_type=F32)
 
-    sent += gather(hb, lambda zt, xt: xt * 4 + zt, lambda zt: hb.at[own], ssem_h, rsem_h, z, x, sent_own, ready, consume)
+    sent += gather(hb, lambda zt, xt: xt * 4 + zt, lambda zt: hb.at[own], ssem_h, rsem_h, z, x, ready, consume)
     halves, half = mbuf.shape[0], mbuf.shape[2]
 
     def m_send(f, xt, target, i):
@@ -408,29 +404,44 @@
         m_send(f, x, cx, 1)
     loads[1 + tiles].wait()
 
-    def down_block(f, zt):
-        lanes = pl.ds(pl.multiple_of(zt * 256, 256), 256)
-        width = mbuf.shape[3]
-        return functools.reduce(lambda a, b: a + b, [
-            jnp.dot(mbuf[f, i], wd[i * width:(i + 1) * width, lanes], preferred_element_type=F32) for i in range(4)])
+    width = mbuf.shape[3]
+
+    def down(lhs, xt, lanes):
+        return jnp.dot(lhs, wd[pl.ds(pl.multiple_of(xt * width, 128), width), lanes], preferred_element_type=F32)
+
+    for xt in (x, cx):
+        if xt is cx:
+            for f in range(halves):
+                m_arrived(f, cx)
+        lhs = jnp.concatenate([mbuf[f, xt] for f in range(halves)], axis=0)
+        for n in range(4):
+            lanes = slice(n * 256, (n + 1) * 256)
+            new = down(lhs, xt, lanes)
+            low[:, lanes] = new if xt is x else low[:, lanes] + new
 
     for f in range(halves):
+        rows = slice(f * half, (f + 1) * half)
         m_arrived(f, yx)
         m_send(f, yx, cx, 2)
-        m_arrived(f, cx)
+        for n in range(4):
+            lanes = slice(n * 256, (n + 1) * 256)
+            low[rows, lanes] += down(mbuf[f, yx], yx, lanes)
         m_arrived(f, cyx)
-        for i, zt in enumerate(reversed(near)):
-            part2[f, zt] = down_block(f, zt).astype(BF)
+
+        for n in range(4):
+            lanes = slice(n * 256, (n + 1) * 256)
+            low[rows, lanes] += down(mbuf[f, cyx], cyx, lanes)
+        for i, zt in enumerate(near):
+            part2[f, zt] = low[rows, block(zt)].astype(BF)
             cp = remote(part2.at[f, zt], recv2.at[f, z], ssem_q.at[f, i], rsem_q.at[f, z], zt, x)
             cp.start()
             sent.append(cp)
-        total2[f] = down_block(f, z)
     for f in range(halves):
-        total = total2[f]
+        rows = slice(f * half, (f + 1) * half)
+        total = low[rows, block(z)]
         for zt in near:
             remote(recv2.at[f, zt], recv2.at[f, zt], ssem_q.at[f, 0], rsem_q.at[f, zt], z, x).wait_recv()
             total += recv2[f, zt].astype(F32)
-        rows = slice(f * half, (f + 1) * half)
         out_ref[rows, :] = (hb[own, rows, :].astype(F32) + total).astype(BF)
     for cp in sent:
         cp.wait_send()
@@ -478,11 +489,11 @@
             out_specs=vmem,
             scratch_shapes=[pltpu.VMEM((4, 8, 8, 128), BF), pltpu.VMEM((128, 256), BF), pltpu.VMEM((1, 4096), BF),
                             pltpu.VMEM((1024, 1024), BF), pltpu.VMEM((7, 8192, 128), BF), pltpu.VMEM((3584, 1024), BF),
-                            pltpu.VMEM((2, 256, 512), BF), pltpu.VMEM((16, 8, 8, 128), BF), pltpu.VMEM((128, 1024), BF),
+                            pltpu.VMEM((256, 1024), BF), pltpu.VMEM((16, 8, 8, 128), BF), pltpu.VMEM((128, 1024), BF),
                             pltpu.VMEM((4, 128, 256), BF), pltpu.VMEM((4, 128, 256), BF), pltpu.VMEM((16, 128, 256), BF),
                             pltpu.VMEM((256, 896), F32), pltpu.VMEM((128, 1), F32), pltpu.VMEM((16, 1, 128), F32),
-                            pltpu.VMEM((2, 4, 64, 896), BF),
-                            pltpu.VMEM((2, 4, 64, 256), BF), pltpu.VMEM((2, 4, 64, 256), BF), pltpu.VMEM((2, 64, 256), F32),
+                            pltpu.VMEM((2, 4, 64, 896), BF), pltpu.VMEM((128, 1024), F32),
+                            pltpu.VMEM((2, 4, 64, 256), BF), pltpu.VMEM((2, 4, 64, 256), BF),
                             dma((12,)), dma((16,)), dma((16,)), dma((15,)), dma((16,)), dma((3,)), dma((4,)), dma((15,)), dma((16,)),
                             dma((2, 3)), dma((2, 4)), dma((2, 3)), dma((2, 4))],
             compiler_params=pltpu.CompilerParams(collective_id=1, has_side_effects=True, vmem_limit_bytes=48 * MIB),

time: 86.9 us -> 81.5 us (0.938)
  Pallas kernels: 83.7 us -> 78.4 us
    pallas_call x1, Pallas kernels: 49.7 us -> 44.9 us  [layer(): pl.pallas_call(mlp_kernel, out_shape=sd(hidden.shape, BF), in_specs=[hbm]...]
where the time goes in v5:
time: 81.5 us; the launch traced here: 81.3 us
  Pallas kernels  78.4 us (96%)
  local copies, waits for them, and re-layouts  2.21 us (3%)
    pallas_call x1, Pallas kernels, layer(): pl.pallas_call(mlp_kernel, out_shape=sd(hidden.shape, BF), in_specs=[hbm]...  44.9 us
    pallas_call x1, Pallas kernels, layer(): pl.pallas_call(qkv_kernel, out_shape=sd((16, 8, 384), BF), in_specs=[hbm,...  24.9 us
    pallas_call x1, Pallas kernels, layer(): pl.pallas_call(attn_kernel, out_shape=(sd((4, 8, rows, hd), BF), sd(k_cac...  8.57 us
    unnamed x15, local copies, waits for them, and re-layouts  2.21 us

profile of v5, /device:TPU:0, one launch (start us, length us, event | category | flops | bytes accessed | tf_op | source)
XLA Modules:
  0.0 81.3 jit_solution(9676863424979971984)
XLA Ops:
  0.6 0.0 copy-start.2
  0.6 0.8 %copy-done.2 = bf16[128,256]{1,0:T(8,128)(2,1)S(1)} copy-done((bf16[128,256]{1,0:T(8,128)(2,1)S(1)}, bf16[128,256]{1,0:T(8,128)(2,1)}, u32[]{:S(2)}) %copy-start.2) | copy-done | bytes 65560
  1.5 0.0 copy-start.6
  1.5 0.7 copy-done.6
  2.2 0.0 copy-start
  2.2 0.0 copy-start.1
  2.2 0.0 copy-start.5
  2.2 24.9 %qkv.1.z_ref = bf16[16,8,384]{2,1,0:T(8,128)(2,1)S(1)} custom-call(bf16[128,256]{1,0:T(8,128)(2,1)S(1)} %copy-done.2, bf16[1,4096]{1,0:T(2,128)(2,1)S(1)} %copy-done.6, bf16[1,1088,4096]{2,1,0:T(8,128)(2,1)} %bitcast.1), custom_call_target="tpu_custom_call" | custom-call | flops 30000001024 | bytes 20000000 | tf_op jit(solution)/shard_map/qkv/pallas_call | solution.py:461
  27.1 0.0 copy-done
  27.1 0.0 copy-done.1
  27.1 0.0 copy-done.5
  27.1 0.0 copy-start.3
  27.1 0.0 copy-start.4
  27.2 8.6 %attend.1 = (bf16[4,8,8,128]{3,2,1,0:T(8,128)(2,1)S(1)}, bf16[1,8,4096,128]{3,2,1,0:T(8,128)(2,1)}, bf16[1,8,4096,128]{3,2,1,0:T(8,128)(2,1)}) custom-call(s32[8]{0:T(128)S(1)} %copy-done.5, bf16[16,8,384]{2,1,0:T(8,128)(2,1)S(1)} %qkv.1.z_ref, bf16[1,8,4096,128]{3,2,1,0:T(8,128)(2,1)S(1)} %copy-done, bf16[1,8,4096,128]{3,2,1,0:T(8,128)(2,1)S(1)} %copy-done.1), custom_call_target="tpu_custom_call" | custom-call | tf_op jit(solution)/shard_map/attend/pallas_call | solution.py:475
  35.7 0.0 copy-done.3
  35.7 0.0 copy-done.4
  35.8 44.9 %mlp.1 = bf16[128,256]{1,0:T(8,128)(2,1)S(1)} custom-call(bf16[4,8,8,128]{3,2,1,0:T(8,128)(2,1)S(1)} %get-tuple-element.6.o_hbm, bf16[128,256]{1,0:T(8,128)(2,1)S(1)} %copy-done.3, bf16[1,4096]{1,0:T(2,128)(2,1)S(1)} %copy-done.4, bf16[1,1024,4096]{2,1,0:T(8,128)(2,1)} %wo_hbm.1, bf16[1,4096,2,3584]{3,2,1,0:T(2,128)(2,1)} %wg_hbm.1, ...), custom_call_target="tpu_custom_call" | custom-call | tf_op jit(solution)/shard_map/mlp/pallas_call | solution.py:485
  80.7 0.6 copy.14
Async XLA Ops:
  0.6 0.8 %copy-start.2 = (bf16[128,256]{1,0:T(8,128)(2,1)S(1)}, bf16[128,256]{1,0:T(8,128)(2,1)}, u32[]{:S(2)}) copy-start(bf16[128,256]{1,0:T(8,128)(2,1)} %h_hbm.3) | copy-start | bytes 196612
  1.5 0.7 copy-start.6
  2.2 24.9 %copy-start = (bf16[1,8,4096,128]{3,2,1,0:T(8,128)(2,1)S(1)}, bf16[1,8,4096,128]{3,2,1,0:T(8,128)(2,1)}, u32[]{:S(2)}) copy-start(bf16[1,8,4096,128]{3,2,1,0:T(8,128)(2,1)} %k_ref.1) | copy-start | bytes 25165828
  2.2 24.9 %copy-start.1 = (bf16[1,8,4096,128]{3,2,1,0:T(8,128)(2,1)S(1)}, bf16[1,8,4096,128]{3,2,1,0:T(8,128)(2,1)}, u32[]{:S(2)}) copy-start(bf16[1,8,4096,128]{3,2,1,0:T(8,128)(2,1)} %v_ref.1) | copy-start | bytes 25165828
  2.2 24.9 %copy-start.5 = (s32[8]{0:T(128)S(1)}, s32[8]{0:T(128)}, u32[]{:S(2)}) copy-start(s32[8]{0:T(128)} %len_ref.1) | copy-start | bytes 100
  27.1 8.6 %copy-start.3 = (bf16[128,256]{1,0:T(8,128)(2,1)S(1)}, bf16[128,256]{1,0:T(8,128)(2,1)}, u32[]{:S(2)}) copy-start(bf16[128,256]{1,0:T(8,128)(2,1)} %h_hbm.3) | copy-start | bytes 196612
  27.1 8.6 %copy-start.4 = (bf16[1,4096]{1,0:T(2,128)(2,1)S(1)}, bf16[1,4096]{1,0:T(2,128)(2,1)}, u32[]{:S(2)}) copy-start(bf16[1,4096]{1,0:T(2,128)(2,1)} %gain_hbm.3) | copy-start | bytes 24580

commit v6 on v5

--- a/solution.py
+++ b/solution.py
@@ -12,7 +12,8 @@
 BF = jnp.bfloat16
 F32 = jnp.float32
 MIB = 1024 * 1024
-UNROLL = 2
+GROUP = 4
+CHUNK = 1024
 
 
 def at(z, x):
@@ -47,11 +48,13 @@
     return n1, n2, 6 - z - n1 - n2
 
 
-def gather(buf, slot, src_for, ssem, rsem, z, x, ready, consume):
+def gather(buf, slot, src, ssem, rsem, z, x, ready, consume):
     yx = lax.rem(x + 2, 4)
     cx = x + 1 - 2 * lax.rem(x, 2)
     cyx = lax.rem(cx + 2, 4)
-    n1, n2, n3 = near = by_distance(z)
+    n1, n2 = 1 + lax.rem(z, 2), 3 * (1 - lax.div(z, 2))
+    n3 = 6 - z - n1 - n2
+    end = 1 - lax.div(z * (3 - z), 2)
     me = slot(z, x)
     started = []
 
@@ -74,12 +77,19 @@
             arrived(slot(zt, xt))
         consume(slot(*first), slot(*second))
 
-    send(src_for(z), me, z, yx)
-    for zt in near:
-        send(src_for(zt), me, zt, x)
-    send(src_for(z), me, z, cx)
+    send(src, me, z, yx)
+    send(src, me, end * n2 + (1 - end) * n1, x)
+    send(src, me, n3, x)
+    third = slot(end * z + (1 - end) * n1, x)
+    third = remote(buf.at[third], buf.at[third], ssem.at[len(started)], rsem.at[third], end * n1 + (1 - end) * n3, x)
+    started.append(third)
+    pl.when(end == 1)(third.start)
+    send(src, me, z, cx)
     pass_on(z, yx, cx)
-    pass_on(n1, x, yx, cx)
+    arrived(slot(n1, x))
+    pl.when(end == 0)(third.start)
+    for t in (yx, cx):
+        send(buf.at[slot(n1, x)], slot(n1, x), z, t)
     ready()
     work((z, x), (z, yx))
     pass_on(n2, x, yx, cx)
@@ -164,7 +174,7 @@
         w = jnp.concatenate([wbuf[:, pl.ds(pl.multiple_of(g * 256, 256), 256)] for g in pair], axis=1)
         acc[...] += lax.dot_general(u, w, (((1,), (1,)), ((), ())), preferred_element_type=F32)
 
-    sent = gather(hb, lambda zt, xt: xt * 4 + zt, lambda zt: h_ref, ssem, rsem, z, x, ready, consume)
+    sent = gather(hb, lambda zt, xt: xt * 4 + zt, h_ref, ssem, rsem, z, x, ready, consume)
     for d in range(16):
         zloc[d] = acc[d * 8:(d + 1) * 8, :].astype(BF)
 
@@ -190,7 +200,7 @@
     out_ref[...] = zbuf[...]
 
 
-def attn_kernel(len_ref, z_ref, k_ref, v_ref, o_ref, ko_hbm, vo_hbm, zrow, orow, tiles, osem, tsem):
+def attn_kernel(len_ref, z_ref, k_ref, v_ref, o_ref, ko_hbm, vo_hbm, zrow, orow, tiles, qrow, score, osem, tsem):
     rows, positions, hd = k_ref.shape[1:]
 
     def store(b, which):
@@ -239,41 +249,55 @@
 
     lax.fori_loop(0, rows, renew, 0)
 
-    def one(b):
-        pos = len_ref[b]
-        k_new, v_new = zrow[b, heads:heads + 1, :], zrow[b, heads + 1:heads + 2, :]
-        q = zrow[b, 0:heads, :]
-        s = lax.dot_general(q.astype(BF), k_ref[0, b], (((1,), (1,)), ((), ())), preferred_element_type=F32)
-        s_new = jnp.sum(q * k_new, axis=1, keepdims=True)
-        ids = lax.broadcasted_iota(jnp.int32, s.shape, 1)
-        s = jnp.where(ids < pos, s, -1e30)
-        top = jnp.maximum(jnp.max(s, axis=1, keepdims=True), s_new)
-        e = jnp.exp2((s - top) * factor)
+    qrow[...] = jnp.zeros_like(qrow)
+    lane_row = lax.broadcasted_iota(jnp.int32, (1, GROUP * heads), 1)
+    nt = (((1,), (1,)), ((), ()))
+
+    def one(g, c):
+        b0 = g * GROUP
+        ends = jnp.zeros((1, GROUP * heads), jnp.int32)
+        for i in range(GROUP):
+            qrow[i * heads:(i + 1) * heads, i * hd:(i + 1) * hd] = zrow[b0 + i, 0:heads, :].astype(BF)
+            ends = jnp.where(lax.div(lane_row, heads) == i, len_ref[b0 + i], ends)
+        q = qrow[...]
+        k_new = jnp.concatenate([jnp.broadcast_to(zrow[b0 + i, heads:heads + 1, :], (8, hd)) for i in range(GROUP)], axis=1)
+        s_new = lax.dot_general(k_new.astype(BF), q, nt, preferred_element_type=F32)[0:1, :]
+        top = s_new
+        for lo in range(0, positions, CHUNK):
+            k = jnp.concatenate([k_ref[0, b0 + i, lo:lo + CHUNK, :] for i in range(GROUP)], axis=1)
+            s = lax.dot_general(k, q, nt, preferred_element_type=F32)
+            ids = lax.broadcasted_iota(jnp.int32, s.shape, 0) + lo
+            s = jnp.where(ids < ends, s, -1e30)
+            score[lo:lo + CHUNK, :] = s
+            top = jnp.maximum(top, jnp.max(s, axis=0, keepdims=True))
         e_new = jnp.exp2((s_new - top) * factor)
-        inv = 1.0 / (jnp.sum(e, axis=1, keepdims=True) + e_new)
-        p = (e * inv).astype(BF)
-        p_new = (e_new * inv).astype(BF).astype(F32)
-        orow[b] = jnp.dot(p, v_ref[0, b], preferred_element_type=F32) + p_new * v_new
+        total = e_new
+        for lo in range(0, positions, CHUNK):
+            e = jnp.exp2((score[lo:lo + CHUNK, :] - top) * factor)
+            score[lo:lo + CHUNK, :] = e
+            total += jnp.sum(e, axis=0, keepdims=True)
+        inv = 1.0 / total
+        p_new = jnp.transpose(jnp.broadcast_to((e_new * inv).astype(BF).astype(F32), (GROUP * heads, GROUP * heads)))
+        outs = [p_new[i * heads:(i + 1) * heads, 0:1] * zrow[b0 + i, heads + 1:heads + 2, :] for i in range(GROUP)]
+        for lo in range(0, positions, CHUNK):
+            p = jnp.transpose((score[lo:lo + CHUNK, :] * inv).astype(BF))
+            for i in range(GROUP):
+                outs[i] += jnp.dot(p[i * heads:(i + 1) * heads, :], v_ref[0, b0 + i, lo:lo + CHUNK, :], preferred_element_type=F32)
+        for i in range(GROUP):
+            orow[b0 + i] = outs[i]
+        return c
 
     def fix(b):
         for which in range(2):
             store(b, which).wait()
             patch(b, which).start()
 
-    def body(i, c):
-        for k in range(UNROLL):
-            one(i * UNROLL + k)
-        return c
-
     def patches(b, c):
         fix(b)
         return c
 
-    lax.fori_loop(0, rows // UNROLL - 1, body, 0)
-    for b in range(rows - UNROLL, rows - 1):
-        one(b)
+    lax.fori_loop(0, rows // GROUP, one, 0)
     lax.fori_loop(0, rows, patches, 0)
-    one(rows - 1)
     for h in range(heads):
         o_ref[h // 8, h % 8] = orow[:, h, :].astype(BF)
 
@@ -385,7 +409,7 @@
                 for g in pair], axis=0)
             acc[:, j * 128:(j + width) * 128] += jnp.dot(lhs, w, preferred_element_type=F32)
 
-    sent += gather(hb, lambda zt, xt: xt * 4 + zt, lambda zt: hb.at[own], ssem_h, rsem_h, z, x, ready, consume)
+    sent += gather(hb, lambda zt, xt: xt * 4 + zt, hb.at[own], ssem_h, rsem_h, z, x, ready, consume)
     halves, half = mbuf.shape[0], mbuf.shape[2]
 
     def m_send(f, xt, target, i):
@@ -470,7 +494,7 @@
             compiler_params=pltpu.CompilerParams(collective_id=0, has_side_effects=True, vmem_limit_bytes=46 * MIB),
             cost_estimate=pl.CostEstimate(flops=30_000_000_000, bytes_accessed=20_000_000, transcendentals=0),
             name="qkv",
-        )(hidden, attn_gain, w_qkv_t)
+        )(pltpu.with_memory_space_constraint(hidden, pltpu.HBM), pltpu.with_memory_space_constraint(attn_gain, pltpu.HBM), w_qkv_t)
         rows, positions, hd = k_cache.shape[1:]
         o, k_out, v_out = pl.pallas_call(
             attn_kernel,
@@ -478,7 +502,8 @@
             in_specs=[smem, vmem, vmem, vmem],
             out_specs=(vmem, hbm, hbm),
             scratch_shapes=[pltpu.VMEM((rows, 34, hd), F32), pltpu.VMEM((rows, 32, hd), F32),
-                            pltpu.VMEM((2, rows, 16, hd), BF), dma((2, rows)), dma((2, rows))],
+                            pltpu.VMEM((2, rows, 16, hd), BF), pltpu.VMEM((GROUP * 32, GROUP * hd), BF),
+                            pltpu.VMEM((positions, GROUP * 32), F32), dma((2, rows)), dma((2, rows))],
             compiler_params=pltpu.CompilerParams(vmem_limit_bytes=28 * MIB),
             name="attend",
         )(seq_lens, z_rows, k_cache, v_cache)

time: 81.5 us -> 79.9 us (0.980)
  local copies, waits for them, and re-layouts: 2.21 us -> 0.66 us
    unnamed x15 -> x11, local copies, waits for them, and re-layouts: 2.21 us -> 0.66 us
    pallas_call x1, Pallas kernels: 44.9 us -> 46.4 us  [layer(): pl.pallas_call(mlp_kernel, out_shape=sd(hidden.shape, BF), in_specs=[hbm]...]
    pallas_call x1, Pallas kernels: 8.57 us -> 7.24 us  [layer(): pl.pallas_call(attn_kernel, out_shape=(sd((4, 8, rows, hd), BF), sd(k_cac...]
where the time goes in v6:
time: 79.9 us; the launch traced here: 79.8 us
  Pallas kernels  78.4 us (98%)
    pallas_call x1, Pallas kernels, layer(): pl.pallas_call(mlp_kernel, out_shape=sd(hidden.shape, BF), in_specs=[hbm]...  46.4 us
    pallas_call x1, Pallas kernels, layer(): pl.pallas_call(qkv_kernel, out_shape=sd((16, 8, 384), BF), in_specs=[hbm,...  24.7 us
    pallas_call x1, Pallas kernels, layer(): pl.pallas_call(attn_kernel, out_shape=(sd((4, 8, rows, hd), BF), sd(k_cac...  7.24 us

profile of v6, /device:TPU:0, one launch (start us, length us, event | category | flops | bytes accessed | tf_op | source)
XLA Modules:
  0.0 79.8 jit_solution(1544796433171376139)
XLA Ops:
  0.6 0.0 copy-start
  0.6 0.0 copy-start.1
  0.7 0.0 copy-start.4
  0.7 24.7 %qkv.1.z_ref = bf16[16,8,384]{2,1,0:T(8,128)(2,1)S(1)} custom-call(bf16[128,256]{1,0:T(8,128)(2,1)} %h_hbm.3, bf16[1,4096]{1,0:T(2,128)(2,1)} %gain_hbm.2, bf16[1,1088,4096]{2,1,0:T(8,128)(2,1)} %bitcast.1), custom_call_target="tpu_custom_call" | custom-call | flops 30000001024 | bytes 20000000 | tf_op jit(solution)/shard_map/qkv/pallas_call | solution.py:485
  25.4 0.0 copy-done
  25.4 0.0 copy-done.1
  25.4 0.0 copy-done.4
  25.4 0.0 copy-start.2
  25.5 0.0 copy-start.3
  25.5 7.2 %attend.1 = (bf16[4,8,8,128]{3,2,1,0:T(8,128)(2,1)S(1)}, bf16[1,8,4096,128]{3,2,1,0:T(8,128)(2,1)}, bf16[1,8,4096,128]{3,2,1,0:T(8,128)(2,1)}) custom-call(s32[8]{0:T(128)S(1)} %copy-done.4, bf16[16,8,384]{2,1,0:T(8,128)(2,1)S(1)} %qkv.1.z_ref, bf16[1,8,4096,128]{3,2,1,0:T(8,128)(2,1)S(1)} %copy-done, bf16[1,8,4096,128]{3,2,1,0:T(8,128)(2,1)S(1)} %copy-done.1), custom_call_target="tpu_custom_call" | custom-call | tf_op jit(solution)/shard_map/attend/pallas_call | solution.py:499
  32.7 0.0 copy-done.2
  32.7 0.0 copy-done.3
  32.7 46.4 %mlp.1 = bf16[128,256]{1,0:T(8,128)(2,1)S(1)} custom-call(bf16[4,8,8,128]{3,2,1,0:T(8,128)(2,1)S(1)} %get-tuple-element.6.o_hbm, bf16[128,256]{1,0:T(8,128)(2,1)S(1)} %copy-done.2, bf16[1,4096]{1,0:T(2,128)(2,1)S(1)} %copy-done.3, bf16[1,1024,4096]{2,1,0:T(8,128)(2,1)} %wo_hbm.1, bf16[1,4096,2,3584]{3,2,1,0:T(2,128)(2,1)} %wg_hbm.1, ...), custom_call_target="tpu_custom_call" | custom-call | tf_op jit(solution)/shard_map/mlp/pallas_call | solution.py:510
  79.2 0.6 copy.14
Async XLA Ops:
  0.6 24.8 %copy-start = (bf16[1,8,4096,128]{3,2,1,0:T(8,128)(2,1)S(1)}, bf16[1,8,4096,128]{3,2,1,0:T(8,128)(2,1)}, u32[]{:S(2)}) copy-start(bf16[1,8,4096,128]{3,2,1,0:T(8,128)(2,1)} %k_ref.1) | copy-start | bytes 25165828
  0.6 24.8 %copy-start.1 = (bf16[1,8,4096,128]{3,2,1,0:T(8,128)(2,1)S(1)}, bf16[1,8,4096,128]{3,2,1,0:T(8,128)(2,1)}, u32[]{:S(2)}) copy-start(bf16[1,8,4096,128]{3,2,1,0:T(8,128)(2,1)} %v_ref.1) | copy-start | bytes 25165828
  0.7 24.8 %copy-start.4 = (s32[8]{0:T(128)S(1)}, s32[8]{0:T(128)}, u32[]{:S(2)}) copy-start(s32[8]{0:T(128)} %len_ref.1) | copy-start | bytes 100
  25.4 7.3 %copy-start.2 = (bf16[128,256]{1,0:T(8,128)(2,1)S(1)}, bf16[128,256]{1,0:T(8,128)(2,1)}, u32[]{:S(2)}) copy-start(bf16[128,256]{1,0:T(8,128)(2,1)} %h_hbm.3) | copy-start | bytes 196612
  25.5 7.3 %copy-start.3 = (bf16[1,4096]{1,0:T(2,128)(2,1)S(1)}, bf16[1,4096]{1,0:T(2,128)(2,1)}, u32[]{:S(2)}) copy-start(bf16[1,4096]{1,0:T(2,128)(2,1)} %gain_hbm.3) | copy-start | bytes 24580

commit v7 on v6

--- a/solution.py
+++ b/solution.py
@@ -328,12 +328,11 @@
     loads.append(pltpu.make_async_copy(wd_hbm.at[0, :, cols], wd, wsem.at[1 + tiles]))
     for cp in loads:
         cp.start()
-    k_id = lax.broadcasted_iota(jnp.int32, (256, 1024), 0)
-    c_id = lax.broadcasted_iota(jnp.int32, (256, 1024), 1)
-    spread[...] = jnp.where(c_id == 2 * k_id + (c_id // 512) * 513, 1.0, 0.0).astype(BF)
-    acc[...] = jnp.zeros_like(acc)
-
     def settle():
+        k_id = lax.broadcasted_iota(jnp.int32, (256, 1024), 0)
+        c_id = lax.broadcasted_iota(jnp.int32, (256, 1024), 1)
+        spread[...] = jnp.where(c_id == 2 * k_id + (c_id // 512) * 513, 1.0, 0.0).astype(BF)
+        acc[...] = jnp.zeros_like(acc)
         for cp in small:
             cp.wait()
 
@@ -410,7 +409,7 @@
             acc[:, j * 128:(j + width) * 128] += jnp.dot(lhs, w, preferred_element_type=F32)
 
     sent += gather(hb, lambda zt, xt: xt * 4 + zt, hb.at[own], ssem_h, rsem_h, z, x, ready, consume)
-    halves, half = mbuf.shape[0], mbuf.shape[2]
+    pieces, half = mbuf.shape[0], mbuf.shape[2]
 
     def m_send(f, xt, target, i):
         cp = remote(mbuf.at[f, xt], mbuf.at[f, xt], ssem_m.at[f, i], rsem_m.at[f, xt], z, target)
@@ -420,7 +419,7 @@
     def m_arrived(f, xt):
         remote(mbuf.at[f, xt], mbuf.at[f, xt], ssem_m.at[f, 0], rsem_m.at[f, xt], z, x).wait_recv()
 
-    for f in range(halves):
+    for f in range(pieces):
         gate = acc[f * half:(f + 1) * half, :].astype(BF).astype(F32)
         up = acc[128 + f * half:128 + (f + 1) * half, :].astype(BF).astype(F32)
         mbuf[f, x] = (jax.nn.silu(gate) * up).astype(BF)
@@ -435,32 +434,33 @@
 
     for xt in (x, cx):
         if xt is cx:
-            for f in range(halves):
+            for f in range(pieces):
                 m_arrived(f, cx)
-        lhs = jnp.concatenate([mbuf[f, xt] for f in range(halves)], axis=0)
+        lhs = jnp.concatenate([mbuf[f, xt] for f in range(pieces)], axis=0)
         for n in range(4):
             lanes = slice(n * 256, (n + 1) * 256)
             new = down(lhs, xt, lanes)
             low[:, lanes] = new if xt is x else low[:, lanes] + new
 
-    for f in range(halves):
-        rows = slice(f * half, (f + 1) * half)
+    def m_pass(f):
         m_arrived(f, yx)
         m_send(f, yx, cx, 2)
+
+    m_pass(0)
+    for f in range(pieces):
+        rows = slice(f * half, (f + 1) * half)
+        if f + 1 < pieces:
+            m_pass(f + 1)
+        m_arrived(f, cyx)
         for n in range(4):
             lanes = slice(n * 256, (n + 1) * 256)
-            low[rows, lanes] += down(mbuf[f, yx], yx, lanes)
-        m_arrived(f, cyx)
-
-        for n in range(4):
-            lanes = slice(n * 256, (n + 1) * 256)
-            low[rows, lanes] += down(mbuf[f, cyx], cyx, lanes)
+            low[rows, lanes] += down(mbuf[f, yx], yx, lanes) + down(mbuf[f, cyx], cyx, lanes)
         for i, zt in enumerate(near):
             part2[f, zt] = low[rows, block(zt)].astype(BF)
             cp = remote(part2.at[f, zt], recv2.at[f, z], ssem_q.at[f, i], rsem_q.at[f, z], zt, x)
             cp.start()
             sent.append(cp)
-    for f in range(halves):
+    for f in range(pieces):
         rows = slice(f * half, (f + 1) * half)
         total = low[rows, block(z)]
         for zt in near:
@@ -517,10 +517,10 @@
                             pltpu.VMEM((256, 1024), BF), pltpu.VMEM((16, 8, 8, 128), BF), pltpu.VMEM((128, 1024), BF),
                             pltpu.VMEM((4, 128, 256), BF), pltpu.VMEM((4, 128, 256), BF), pltpu.VMEM((16, 128, 256), BF),
                             pltpu.VMEM((256, 896), F32), pltpu.VMEM((128, 1), F32), pltpu.VMEM((16, 1, 128), F32),
-                            pltpu.VMEM((2, 4, 64, 896), BF), pltpu.VMEM((128, 1024), F32),
-                            pltpu.VMEM((2, 4, 64, 256), BF), pltpu.VMEM((2, 4, 64, 256), BF),
+                            pltpu.VMEM((4, 4, 32, 896), BF), pltpu.VMEM((128, 1024), F32),
+                            pltpu.VMEM((4, 4, 32, 256), BF), pltpu.VMEM((4, 4, 32, 256), BF),
                             dma((12,)), dma((16,)), dma((16,)), dma((15,)), dma((16,)), dma((3,)), dma((4,)), dma((15,)), dma((16,)),
-                            dma((2, 3)), dma((2, 4)), dma((2, 3)), dma((2, 4))],
+                            dma((4, 3)), dma((4, 4)), dma((4, 3)), dma((4, 4))],
             compiler_params=pltpu.CompilerParams(collective_id=1, has_side_effects=True, vmem_limit_bytes=48 * MIB),
             name="mlp",
         )(o, hidden, mlp_gain, w_out, w_gate_up, w_down)

time: 79.9 us -> 78.8 us (0.986)
  Pallas kernels: 78.4 us -> 77.3 us
    pallas_call x1, Pallas kernels: 46.4 us -> 45.3 us  [layer(): pl.pallas_call(mlp_kernel, out_shape=sd(hidden.shape, BF), in_specs=[hbm]...]
where the time goes in v7:
time: 78.8 us; the launch traced here: 78.7 us
  Pallas kernels  77.3 us (98%)
    pallas_call x1, Pallas kernels, layer(): pl.pallas_call(mlp_kernel, out_shape=sd(hidden.shape, BF), in_specs=[hbm]...  45.3 us
    pallas_call x1, Pallas kernels, layer(): pl.pallas_call(qkv_kernel, out_shape=sd((16, 8, 384), BF), in_specs=[hbm,...  24.7 us
    pallas_call x1, Pallas kernels, layer(): pl.pallas_call(attn_kernel, out_shape=(sd((4, 8, rows, hd), BF), sd(k_cac...  7.24 us

profile of v7, /device:TPU:0, one launch (start us, length us, event | category | flops | bytes accessed | tf_op | source)
XLA Modules:
  0.0 78.7 jit_solution(8344508792065195518)
XLA Ops:
  0.6 0.0 copy-start
  0.6 0.0 copy-start.1
  0.7 0.0 copy-start.4
  0.7 24.7 %qkv.1.z_ref = bf16[16,8,384]{2,1,0:T(8,128)(2,1)S(1)} custom-call(bf16[128,256]{1,0:T(8,128)(2,1)} %h_hbm.3, bf16[1,4096]{1,0:T(2,128)(2,1)} %gain_hbm.2, bf16[1,1088,4096]{2,1,0:T(8,128)(2,1)} %bitcast.1), custom_call_target="tpu_custom_call" | custom-call | flops 30000001024 | bytes 20000000 | tf_op jit(solution)/shard_map/qkv/pallas_call | solution.py:485
  25.4 0.0 copy-done
  25.4 0.0 copy-done.1
  25.4 0.0 copy-done.4
  25.4 0.0 copy-start.2
  25.5 0.0 copy-start.3
  25.5 7.2 %attend.1 = (bf16[4,8,8,128]{3,2,1,0:T(8,128)(2,1)S(1)}, bf16[1,8,4096,128]{3,2,1,0:T(8,128)(2,1)}, bf16[1,8,4096,128]{3,2,1,0:T(8,128)(2,1)}) custom-call(s32[8]{0:T(128)S(1)} %copy-done.4, bf16[16,8,384]{2,1,0:T(8,128)(2,1)S(1)} %qkv.1.z_ref, bf16[1,8,4096,128]{3,2,1,0:T(8,128)(2,1)S(1)} %copy-done, bf16[1,8,4096,128]{3,2,1,0:T(8,128)(2,1)S(1)} %copy-done.1), custom_call_target="tpu_custom_call" | custom-call | tf_op jit(solution)/shard_map/attend/pallas_call | solution.py:499
  32.7 0.0 copy-done.2
  32.7 0.0 copy-done.3
  32.7 45.3 %mlp.1 = bf16[128,256]{1,0:T(8,128)(2,1)S(1)} custom-call(bf16[4,8,8,128]{3,2,1,0:T(8,128)(2,1)S(1)} %get-tuple-element.6.o_hbm, bf16[128,256]{1,0:T(8,128)(2,1)S(1)} %copy-done.2, bf16[1,4096]{1,0:T(2,128)(2,1)S(1)} %copy-done.3, bf16[1,1024,4096]{2,1,0:T(8,128)(2,1)} %wo_hbm.1, bf16[1,4096,2,3584]{3,2,1,0:T(2,128)(2,1)} %wg_hbm.1, ...), custom_call_target="tpu_custom_call" | custom-call | tf_op jit(solution)/shard_map/mlp/pallas_call | solution.py:510
  78.0 0.6 copy.14
Async XLA Ops:
  0.6 24.8 %copy-start = (bf16[1,8,4096,128]{3,2,1,0:T(8,128)(2,1)S(1)}, bf16[1,8,4096,128]{3,2,1,0:T(8,128)(2,1)}, u32[]{:S(2)}) copy-start(bf16[1,8,4096,128]{3,2,1,0:T(8,128)(2,1)} %k_ref.1) | copy-start | bytes 25165828
  0.6 24.8 %copy-start.1 = (bf16[1,8,4096,128]{3,2,1,0:T(8,128)(2,1)S(1)}, bf16[1,8,4096,128]{3,2,1,0:T(8,128)(2,1)}, u32[]{:S(2)}) copy-start(bf16[1,8,4096,128]{3,2,1,0:T(8,128)(2,1)} %v_ref.1) | copy-start | bytes 25165828
  0.7 24.8 %copy-start.4 = (s32[8]{0:T(128)S(1)}, s32[8]{0:T(128)}, u32[]{:S(2)}) copy-start(s32[8]{0:T(128)} %len_ref.1) | copy-start | bytes 100
  25.4 7.3 %copy-start.2 = (bf16[128,256]{1,0:T(8,128)(2,1)S(1)}, bf16[128,256]{1,0:T(8,128)(2,1)}, u32[]{:S(2)}) copy-start(bf16[128,256]{1,0:T(8,128)(2,1)} %h_hbm.3) | copy-start | bytes 196612
  25.5 7.3 %copy-start.3 = (bf16[1,4096]{1,0:T(2,128)(2,1)S(1)}, bf16[1,4096]{1,0:T(2,128)(2,1)}, u32[]{:S(2)}) copy-start(bf16[1,4096]{1,0:T(2,128)(2,1)} %gain_hbm.3) | copy-start | bytes 24580

commit v8 on v7

--- a/solution.py
+++ b/solution.py
@@ -146,7 +146,7 @@
 
 
 def qkv_kernel(h_hbm, gain_hbm, w_hbm, out_ref, h_ref, gain, hb, wbuf, acc, scale, stat, zloc, zbuf,
-               wsem, ssem, rsem, ssem_s, rsem_s, ssem2, rsem2):
+               wsem, ssem, rsem, ssem_s, rsem_s, ssem2, rsem2, ssem3, rsem3):
     z, x = lax.axis_index("yz"), lax.axis_index("x")
     me = z * 4 + x
     parts = [
@@ -178,9 +178,13 @@
     for d in range(16):
         zloc[d] = acc[d * 8:(d + 1) * 8, :].astype(BF)
 
+    main, tail, near = pl.ds(0, 256), pl.ds(256, 128), by_distance(z)
+    tails = [remote(zloc.at[zt * 4 + x, :, tail], zbuf.at[me, :, tail], ssem3.at[i], rsem3.at[z], zt, x)
+             for i, zt in enumerate(near)]
+
     def peer(p):
         d = lax.rem(me + p, 16)
-        return remote(zloc.at[d], zbuf.at[me], ssem2.at[p], rsem2.at[me], lax.div(d, 4), lax.rem(d, 4))
+        return remote(zloc.at[d, :, main], zbuf.at[me, :, main], ssem2.at[p], rsem2.at[me], lax.div(d, 4), lax.rem(d, 4))
 
     def start(p, c):
         peer(p).start()
@@ -189,19 +193,26 @@
     def finish(p, c):
         peer(p).wait_send()
         d = lax.rem(me + p, 16)
-        remote(zbuf.at[d], zbuf.at[d], ssem2.at[0], rsem2.at[d], z, x).wait_recv()
+        remote(zbuf.at[d, :, main], zbuf.at[d, :, main], ssem2.at[0], rsem2.at[d], z, x).wait_recv()
         return c
 
     lax.fori_loop(1, 16, start, 0)
+    for cp in tails:
+        cp.start()
     zbuf[me] = zloc[me]
     for cp in sent:
         cp.wait_send()
     lax.fori_loop(1, 16, finish, 0)
+    for cp, zt in zip(tails, near):
+        cp.wait_send()
+        d = zt * 4 + x
+        remote(zbuf.at[d, :, tail], zbuf.at[d, :, tail], ssem3.at[0], rsem3.at[zt], z, x).wait_recv()
     out_ref[...] = zbuf[...]
 
 
 def attn_kernel(len_ref, z_ref, k_ref, v_ref, o_ref, ko_hbm, vo_hbm, zrow, orow, tiles, qrow, score, osem, tsem):
     rows, positions, hd = k_ref.shape[1:]
+    x = lax.axis_index("x")
 
     def store(b, which):
         src, dst = ((k_ref, ko_hbm), (v_ref, vo_hbm))[which]
@@ -226,8 +237,8 @@
         even, odd = 8 * pair, 8 * pair + 4
         mains_e = [z_ref[even + i // 2, :, (i % 2) * hd:(i % 2 + 1) * hd].astype(F32) for i in range(8)]
         mains_o = [pltpu.roll(z_ref[odd + i // 2, :, (i % 2) * hd:(i % 2 + 1) * hd].astype(F32), hd // 2, 1) for i in range(8)]
-        tail_e = z_ref[even, :, 2 * hd:3 * hd].astype(F32)
-        tail_o = z_ref[odd, :, 2 * hd:3 * hd].astype(F32)
+        tail_e = z_ref[even + x, :, 2 * hd:3 * hd].astype(F32)
+        tail_o = z_ref[odd + x, :, 2 * hd:3 * hd].astype(F32)
         heads = mains_e + [jnp.where(lane < hd // 2, tail_e, mains_o[0])]
         for i in range(8):
             heads.append(jnp.where(lane < hd // 2, mains_o[i], mains_o[i + 1] if i < 7 else tail_o))
@@ -490,7 +501,8 @@
             scratch_shapes=[pltpu.VMEM((128, 256), BF), pltpu.VMEM((1, 4096), BF), pltpu.VMEM((16, 128, 256), BF), pltpu.VMEM((384, 4096), BF), pltpu.VMEM((128, 384), F32),
                             pltpu.VMEM((128, 1), F32), pltpu.VMEM((16, 1, 128), F32),
                             pltpu.VMEM((16, 8, 384), BF), pltpu.VMEM((16, 8, 384), BF),
-                            dma((5,)), dma((15,)), dma((16,)), dma((16,)), dma((16,)), dma((16,)), dma((16,))],
+                            dma((5,)), dma((15,)), dma((16,)), dma((16,)), dma((16,)), dma((16,)), dma((16,)),
+                            dma((3,)), dma((4,))],
             compiler_params=pltpu.CompilerParams(collective_id=0, has_side_effects=True, vmem_limit_bytes=46 * MIB),
             cost_estimate=pl.CostEstimate(flops=30_000_000_000, bytes_accessed=20_000_000, transcendentals=0),
             name="qkv",

time: 78.8 us -> 78.5 us (level)
  no operation moved by 1% of the time
where the time goes in v8:
time: 78.5 us; the launch traced here: 78.4 us
  Pallas kernels  77 us (98%)
    pallas_call x1, Pallas kernels, layer(): pl.pallas_call(mlp_kernel, out_shape=sd(hidden.shape, BF), in_specs=[hbm]...  44.9 us
    pallas_call x1, Pallas kernels, layer(): pl.pallas_call(qkv_kernel, out_shape=sd((16, 8, 384), BF), in_specs=[hbm,...  24.8 us
    pallas_call x1, Pallas kernels, layer(): pl.pallas_call(attn_kernel, out_shape=(sd((4, 8, rows, hd), BF), sd(k_cac...  7.25 us

profile of v8, /device:TPU:0, one launch (start us, length us, event | category | flops | bytes accessed | tf_op | source)
XLA Modules:
  0.0 78.4 jit_solution(1134982910625631533)
XLA Ops:
  0.6 0.0 copy-start
  0.6 0.0 copy-start.1
  0.7 0.0 copy-start.4
  0.7 24.8 %qkv.1.z_ref = bf16[16,8,384]{2,1,0:T(8,128)(2,1)S(1)} custom-call(bf16[128,256]{1,0:T(8,128)(2,1)} %h_hbm.3, bf16[1,4096]{1,0:T(2,128)(2,1)} %gain_hbm.2, bf16[1,1088,4096]{2,1,0:T(8,128)(2,1)} %bitcast.1), custom_call_target="tpu_custom_call" | custom-call | flops 30000001024 | bytes 20000000 | tf_op jit(solution)/shard_map/qkv/pallas_call | solution.py:496
  25.4 0.0 copy-done
  25.5 0.0 copy-done.1
  25.5 0.0 copy-done.4
  25.5 0.0 copy-start.2
  25.5 0.0 copy-start.3
  25.5 7.3 %attend.1 = (bf16[4,8,8,128]{3,2,1,0:T(8,128)(2,1)S(1)}, bf16[1,8,4096,128]{3,2,1,0:T(8,128)(2,1)}, bf16[1,8,4096,128]{3,2,1,0:T(8,128)(2,1)}) custom-call(s32[8]{0:T(128)S(1)} %copy-done.4, bf16[16,8,384]{2,1,0:T(8,128)(2,1)S(1)} %qkv.1.z_ref, bf16[1,8,4096,128]{3,2,1,0:T(8,128)(2,1)S(1)} %copy-done, bf16[1,8,4096,128]{3,2,1,0:T(8,128)(2,1)S(1)} %copy-done.1), custom_call_target="tpu_custom_call" | custom-call | tf_op jit(solution)/shard_map/attend/pallas_call | solution.py:511
  32.8 0.0 copy-done.2
  32.8 0.0 copy-done.3
  32.8 44.9 %mlp.1 = bf16[128,256]{1,0:T(8,128)(2,1)S(1)} custom-call(bf16[4,8,8,128]{3,2,1,0:T(8,128)(2,1)S(1)} %get-tuple-element.6.o_hbm, bf16[128,256]{1,0:T(8,128)(2,1)S(1)} %copy-done.2, bf16[1,4096]{1,0:T(2,128)(2,1)S(1)} %copy-done.3, bf16[1,1024,4096]{2,1,0:T(8,128)(2,1)} %wo_hbm.1, bf16[1,4096,2,3584]{3,2,1,0:T(2,128)(2,1)} %wg_hbm.1, ...), custom_call_target="tpu_custom_call" | custom-call | tf_op jit(solution)/shard_map/mlp/pallas_call | solution.py:522
  77.7 0.6 copy.14
Async XLA Ops:
  0.6 24.8 %copy-start = (bf16[1,8,4096,128]{3,2,1,0:T(8,128)(2,1)S(1)}, bf16[1,8,4096,128]{3,2,1,0:T(8,128)(2,1)}, u32[]{:S(2)}) copy-start(bf16[1,8,4096,128]{3,2,1,0:T(8,128)(2,1)} %k_ref.1) | copy-start | bytes 25165828
  0.6 24.8 %copy-start.1 = (bf16[1,8,4096,128]{3,2,1,0:T(8,128)(2,1)S(1)}, bf16[1,8,4096,128]{3,2,1,0:T(8,128)(2,1)}, u32[]{:S(2)}) copy-start(bf16[1,8,4096,128]{3,2,1,0:T(8,128)(2,1)} %v_ref.1) | copy-start | bytes 25165828
  0.7 24.8 %copy-start.4 = (s32[8]{0:T(128)S(1)}, s32[8]{0:T(128)}, u32[]{:S(2)}) copy-start(s32[8]{0:T(128)} %len_ref.1) | copy-start | bytes 100
  25.5 7.3 %copy-start.2 = (bf16[128,256]{1,0:T(8,128)(2,1)S(1)}, bf16[128,256]{1,0:T(8,128)(2,1)}, u32[]{:S(2)}) copy-start(bf16[128,256]{1,0:T(8,128)(2,1)} %h_hbm.3) | copy-start | bytes 196612
  25.5 7.3 %copy-start.3 = (bf16[1,4096]{1,0:T(2,128)(2,1)S(1)}, bf16[1,4096]{1,0:T(2,128)(2,1)}, u32[]{:S(2)}) copy-start(bf16[1,4096]{1,0:T(2,128)(2,1)} %gain_hbm.3) | copy-start | bytes 24580
